TPU v7x, 32 devices: a whole 2x2x4 slice. The times are simulated.
32 devices in a mesh: rep: 4 (over y, core), row: 4 (over z), col: 2 (over x).
Axes of the slice: x: 2, y: 2, z: 4, core: 2. Of those that a mesh axis runs over, the one named last changes fastest.
Arguments:
- patches: bfloat16 [4096, 588], P(('rep', 'col')), may hold values from -20 to 20
- embed_weight: bfloat16 [588, 6144], P(None, 'row'), may hold values from -1 to 1
- embed_bias: float32 [6144], P('row'), may hold values from -3 to 3
- old_in: bfloat16 [64, 768, 1536], P(('row', 'col')), may hold values from -0.078125 to 0.078125
- old_out: bfloat16 [64, 1536, 768], P(('row', 'col')), may hold values from -0.0546875 to 0.0546875
- restore_id: int32 [1], replicated, may hold values from 0 to 47
- norm_gains: float32 [48, 6144], P(None, 'row'), may hold values from 0.1 to 1.9
- in_biases: float32 [48, 12288], P(None, 'col'), may hold values from -3 to 3
- out_biases: float32 [48, 6144], P(None, 'row'), may hold values from -3 to 3
- final_gain: float32 [6144], P('row'), may hold values from 0.1 to 1.9
- check_weight: bfloat16 [6144, 128], P('row'), may hold values from -0.078125 to 0.078125
Outputs:
- in_weight: bfloat16 [6144, 12288], P('row', 'col')
- out_weight: bfloat16 [12288, 6144], P('col', 'row')
- check_logits: float32 [4096, 128], P(('rep', 'col'))
All inputs are finite; a program needn't handle non-finite values.
Results may differ from a plain program's by a relative error of at most 0.0062.
Values may be sent and summed in bfloat16 or wider, within the bound.
A program may use at most 192 MiB of HBM per device.

v0:
```python
import jax
import jax.numpy as jnp
from jax import lax
from jax.sharding import PartitionSpec as P

EPSILON = 1e-06
CHUNKS = 2


def for_sending(shard):
    return jax.tree.map(lambda a: a.astype(jnp.bfloat16) if a.dtype == jnp.float32 else a, shard)


def partner(value, axis, bit):
    mask = 2**bit
    pairs = [(source, source ^ mask) for source in range(lax.axis_size(axis))]
    return lax.ppermute(value, axis, pairs)


def pick_rows(restore_id, param_table):
    selector = (
        jnp.arange(param_table.shape[0], dtype=jnp.int32)[None, :] == restore_id[:, None]
    ).astype(jnp.float32)
    return jnp.dot(selector, param_table, precision=lax.Precision.HIGHEST)[0]


def norm_rows(values, gain_row):
    feature_count = values.shape[1] * lax.axis_size("row")
    totals = lax.psum((jnp.sum(values, axis=1), jnp.sum(values * values, axis=1)), "row")
    average = totals[0][:, None] / feature_count
    spread = totals[1][:, None] / feature_count - average * average
    return ((values - average) * lax.rsqrt(spread + EPSILON) * gain_row).astype(jnp.bfloat16)


def move_halves(pieces, bit_total, device_index, exchange):
    for bit_number in range(bit_total):
        upper_side = device_index >> bit_number & 1 == 1
        outgoing = tuple(
            (jnp.where(upper_side, lower_part, upper_part) for lower_part, upper_part in pieces)
        )
        incoming = exchange(outgoing, bit_number)
        pieces = tuple(
            (
                (
                    jnp.where(upper_side, arrived, lower_part),
                    jnp.where(upper_side, upper_part, arrived),
                )
                for (lower_part, upper_part), arrived in zip(pieces, incoming)
            )
        )
    return pieces


def butterfly_weights(old_in, old_out):
    tiles_here, tile_rows, tile_cols = old_in.shape
    local_cols = tiles_here * tile_cols
    half_cols = local_cols // 2
    in_local = jnp.transpose(old_in, (1, 0, 2)).reshape(tile_rows, local_cols)
    out_local = old_out.reshape(local_cols, tile_rows)
    col_index = lax.axis_index("col")
    col_count = lax.axis_size("col")
    col_bits = col_count.bit_length() - 1
    pieces = (
        (in_local[:, :half_cols], in_local[:, half_cols:]),
        (out_local[:half_cols], out_local[half_cols:]),
    )
    pieces = move_halves(
        pieces,
        col_bits,
        col_index,
        lambda send_parts, bit_number: jax.tree.map(
            lambda part, own: part.astype(own.dtype),
            partner(for_sending(send_parts), "col", bit_number),
            send_parts,
        ),
    )
    in_pair, out_pair = pieces
    in_weight = jnp.concatenate(in_pair, axis=0)
    out_weight = jnp.concatenate(out_pair, axis=1)
    return in_weight, out_weight


def shared_exchange(old_in, old_out):
    tiles_here, tile_rows, tile_cols = old_in.shape
    half_tiles = tiles_here // 2
    half_cols = half_tiles * tile_cols
    col_index = lax.axis_index("col")
    rep_index = lax.axis_index("rep")
    rep_count = lax.axis_size("rep")
    in_parts = old_in.reshape(2, rep_count, half_tiles * tile_rows // rep_count, tile_cols)
    share = lax.dynamic_slice(
        in_parts, (1 - col_index, rep_index, 0, 0), (1, 1) + in_parts.shape[2:]
    )[0, 0]
    share = partner(share, "col", 0)
    out_parts = old_out.reshape(2, half_cols, tile_rows)
    out_sent = lax.dynamic_index_in_dim(out_parts, 1 - col_index, 0, keepdims=False)
    out_kept = lax.dynamic_index_in_dim(out_parts, col_index, 0, keepdims=False)
    share, out_sent = lax.optimization_barrier((share, out_sent))
    out_arrived = partner(out_sent, "col", 0)
    in_arrived = lax.all_gather(share, "rep", axis=0, tiled=True)

    def as_rows(tiles):
        rows = tiles.reshape(half_tiles, tile_rows, tile_cols)
        return jnp.transpose(rows, (1, 0, 2)).reshape(1, tile_rows, half_cols)

    kept = as_rows(lax.dynamic_index_in_dim(in_parts, col_index, 0, keepdims=False))
    blocks = jnp.zeros((2, tile_rows, half_cols), old_in.dtype)
    blocks = lax.dynamic_update_slice(blocks, kept, (col_index, 0, 0))
    blocks = lax.dynamic_update_slice(blocks, as_rows(in_arrived), (1 - col_index, 0, 0))
    return blocks.reshape(2 * tile_rows, half_cols), out_kept, out_arrived


def join_out(out_kept, out_arrived):
    upper_side = lax.axis_index("col") == 1
    return jnp.concatenate(
        (
            jnp.where(upper_side, out_arrived, out_kept),
            jnp.where(upper_side, out_kept, out_arrived),
        ),
        axis=1,
    )


def on_device(
    patches,
    embed_weight,
    embed_bias,
    old_in,
    old_out,
    restore_id,
    norm_gains,
    in_biases,
    out_biases,
    final_gain,
    check_weight,
):
    paired = (
        lax.axis_size("col") == 2
        and old_in.shape[0] % 2 == 0
        and (old_in.shape[0] // 2 * old_in.shape[1]) % lax.axis_size("rep") == 0
    )
    if paired:
        in_weight, out_kept, out_arrived = shared_exchange(old_in, old_out)
    else:
        in_weight, out_weight = butterfly_weights(old_in, old_out)
    layer_gain = pick_rows(restore_id, norm_gains)
    in_bias = pick_rows(restore_id, in_biases)
    out_bias = pick_rows(restore_id, out_biases)
    embedded = jnp.dot(patches, embed_weight, preferred_element_type=jnp.float32) + embed_bias
    normed = norm_rows(embedded, layer_gain)
    tokens = lax.all_gather(normed, "col", axis=0, tiled=True)
    chunk_rows = tokens.shape[0] // CHUNKS
    pre_shares = []
    for chunk in range(CHUNKS):
        partial_pre = jnp.dot(
            tokens[chunk * chunk_rows : (chunk + 1) * chunk_rows],
            in_weight,
            preferred_element_type=jnp.float32,
        ).astype(jnp.bfloat16)
        pre_shares.append(
            lax.psum_scatter(partial_pre, "row", scatter_dimension=0, tiled=True)
        )
    hidden_chunks = [
        jax.nn.gelu(share.astype(jnp.float32) + in_bias, approximate=False).astype(jnp.bfloat16)
        for share in pre_shares
    ]
    if paired:
        hidden_chunks[0], out_arrived = lax.optimization_barrier((hidden_chunks[0], out_arrived))
        out_weight = join_out(out_kept, out_arrived)
    partial_branch = jnp.concatenate(
        [
            jnp.dot(
                lax.all_gather(hidden, "row", axis=0, tiled=True),
                out_weight,
                preferred_element_type=jnp.float32,
            ).astype(jnp.bfloat16)
            for hidden in hidden_chunks
        ],
        axis=0,
    )
    updated = (
        embedded
        + lax.psum_scatter(partial_branch, "col", scatter_dimension=0, tiled=True).astype(jnp.float32)
        + out_bias
    )
    final_normed = norm_rows(updated, final_gain)
    check_logits = lax.psum(
        jnp.dot(final_normed, check_weight, preferred_element_type=jnp.float32), "row"
    )
    return (in_weight, out_weight, check_logits)


def solution(mesh):
    placed = (
        P(("rep", "col"), None),
        P(None, "row"),
        P("row"),
        P(("row", "col"), None, None),
        P(("row", "col"), None, None),
        P(),
        P(None, "row"),
        P(None, "col"),
        P(None, "row"),
        P("row"),
        P("row", None),
    )
    return jax.shard_map(
        on_device,
        mesh=mesh,
        in_specs=placed,
        out_specs=(P("row", "col"), P("col", "row"), P(("rep", "col"), None)),
        check_vma=False,
    )
```

profile of v0, /device:TPU:0, one launch (start us, length us, event | category | flops | bytes accessed | tf_op | source)
XLA Modules:
  0.0 784.1 jit_solution(532455268089544893)
XLA Ops:
  7.2 3.3 dynamic-slice_bitcast_fusion.2
  10.6 3.0 collective-permute-start
  13.6 8.0 %dynamic-slice_bitcast_fusion = bf16[6144,768]{1,0:T(8,128)(2,1)} fusion(bf16[2,6144,768]{2,1,0:T(8,128)(2,1)} %bitcast.50, s32[]{:T(128)S(6)} %select_n.28), kind=kLoop, calls=%fused_computation.3 | loop fusion | bytes 18874372 | tf_op jit(solution)/shard_map/jit(dynamic_index_in_dim)/squeeze | solution.py:96
  21.5 43.6 %collective-permute-done = bf16[768,1536]{1,0:T(8,128)(2,1)} collective-permute-done((bf16[768,1536]{1,0:T(8,128)(2,1)}, bf16[768,1536]{1,0:T(8,128)(2,1)}, u32[]{:S(2)}, u32[]{:S(2)}) %collective-permute-start) | collective-permute-done | bytes 2359328 | tf_op jit(solution)/shard_map/ppermute | solution.py:17
  65.1 0.0 all-gather.7.cloned.1.call-start
  65.9 3.3 fusion.40
  69.2 12.2 %all-reduce.1 = (f32[512]{0:T(512)S(1)}, f32[512]{0:T(512)S(1)}) all-reduce(f32[512]{0:T(512)S(1)} %get-tuple-element.14, f32[512]{0:T(512)S(1)} %get-tuple-element.13), channel_id=1, replica_groups=mesh['rep'=4,'row'=4,'col'=2] {'row'}, use_global_device_ids=true, to_apply=%region_3.4 | all-reduce | flops 1024 | bytes 8192 | tf_op jit(solution)/shard_map/psum | solution.py:29
  81.4 0.2 convolution_reduce_fusion.1
  81.6 3.5 multiply_convert_fusion.1
  85.2 0.0 reduce-scatter.6.cloned.1.call-start
  85.2 8.1 %dynamic-slice_bitcast_fusion.1 = bf16[768,4,1536]{2,0,1:T(8,128)(2,1)} fusion(bf16[2,4,768,1536]{3,2,1,0:T(8,128)(2,1)} %bitcast.54, s32[]{:T(128)S(6)} %select_n.27), kind=kLoop, calls=%fused_computation.4 | loop fusion | bytes 18874372 | tf_op jit(solution)/shard_map/transpose | solution.py:104
  93.4 12.6 %copy.14 = bf16[768,4,1536]{0,2,1:T(8,128)(2,1)} copy(bf16[768,4,1536]{2,0,1:T(8,128)(2,1)} %dynamic-slice_bitcast_fusion.1) | data formatting | bytes 18874368 | tf_op jit(solution)/shard_map/transpose | solution.py:104
  106.0 12.6 %copy.15 = bf16[1,768,6144]{2,1,0:T(8,128)(2,1)} copy(bf16[1,768,6144]{1,2,0:T(8,128)(2,1)} %bitcast.45) | data formatting | bytes 18874368 | tf_op jit(solution)/shard_map/reshape | solution.py:104
  118.6 6.7 broadcast_in_dim.2
  125.3 8.6 %constant_dynamic-update-slice_fusion.1 = bf16[2,768,6144]{2,1,0:T(8,128)(2,1)} fusion(bf16[2,768,6144]{2,1,0:T(8,128)(2,1)} %broadcast_in_dim.2, bf16[1,768,6144]{2,1,0:T(8,128)(2,1)} %copy.15, s32[]{:T(128)S(6)} %select_n.27), kind=kLoop, calls=%fused_computation.77 | loop fusion | bytes 18874372 | tf_op jit(solution)/shard_map/dynamic_update_slice | solution.py:108
  133.9 12.8 %copy.16 = bf16[768,4,1536]{0,2,1:T(8,128)(2,1)} copy(bf16[768,4,1536]{2,0,1:T(8,128)(2,1)} %bitcast.52) | data formatting | bytes 18874368 | tf_op jit(solution)/shard_map/transpose | solution.py:104
  146.7 12.7 %copy.17 = bf16[1,768,6144]{2,1,0:T(8,128)(2,1)} copy(bf16[1,768,6144]{1,2,0:T(8,128)(2,1)} %bitcast.46) | data formatting | bytes 18874368 | tf_op jit(solution)/shard_map/reshape | solution.py:104
  159.4 8.6 %constant_dynamic-update-slice_fusion = bf16[2,768,6144]{2,1,0:T(8,128)(2,1)} fusion(bf16[2,768,6144]{2,1,0:T(8,128)(2,1)} %constant_dynamic-update-slice_fusion.1, bf16[1,768,6144]{2,1,0:T(8,128)(2,1)} %copy.17, s32[]{:T(128)S(6)} %select_n.28), kind=kLoop, calls=%fused_computation.76 | loop fusion | bytes 18874372 | tf_op jit(solution)/shard_map/dynamic_update_slice | solution.py:109
  168.0 9.5 %all-gather.7.cloned.1.call-done = bf16[1024,1536]{1,0:T(8,128)(2,1)} async-done(((bf16[512,1536]{1,0:T(8,128)(2,1)}), bf16[1024,1536]{1,0:T(8,128)(2,1)}) %all-gather.7.cloned.1.call-update) | async-done | bytes 3145744 | tf_op jit(solution)/shard_map/all_gather | solution.py:151
  177.5 15.9 %convolution_convert_fusion = bf16[512,6144]{1,0:T(8,128)(2,1)} fusion(bf16[1536,6144]{1,0:T(8,128)(2,1)} %bitcast.47, bf16[1024,1536]{1,0:T(8,128)(2,1)} %all-gather.7.cloned.1.call-done), kind=kOutput, calls=%fused_computation.5 | convolution fusion | flops 9666822144 | bytes 26738688 | tf_op jit(solution)/shard_map/dot_general | solution.py:155
  193.5 0.2 reduce-scatter.4.cloned.1.call-start
  193.7 16.0 %convolution_convert_fusion.1 = bf16[512,6144]{1,0:T(8,128)(2,1)} fusion(bf16[1536,6144]{1,0:T(8,128)(2,1)} %bitcast.48, bf16[1024,1536]{1,0:T(8,128)(2,1)} %all-gather.7.cloned.1.call-done), kind=kOutput, calls=%fused_computation.6 | convolution fusion | flops 9666822144 | bytes 26738688 | tf_op jit(solution)/shard_map/dot_general | solution.py:155
  209.7 0.0 all-gather.11.cloned.1.call-start
  209.8 1.2 copy-done.3
  211.0 0.5 fusion.34
  211.5 0.4 collective-permute-start.1
  211.9 92.5 %reduce-scatter.6.cloned.1.call-done = bf16[128,6144]{1,0:T(8,128)(2,1)} async-done(((bf16[512,6144]{1,0:T(8,128)(2,1)}), bf16[128,6144]{1,0:T(8,128)(2,1)}) %reduce-scatter.6.cloned.1.call-update) | async-done | bytes 1572880 | tf_op jit(solution)/shard_map/reduce_scatter | solution.py:161
  304.4 113.5 %reduce-scatter.4.cloned.1.call-done = bf16[128,6144]{1,0:T(8,128)(2,1)} async-done(((bf16[512,6144]{1,0:T(8,128)(2,1)}), bf16[128,6144]{1,0:T(8,128)(2,1)}) %reduce-scatter.4.cloned.1.call-update) | async-done | bytes 1572880 | tf_op jit(solution)/shard_map/reduce_scatter | solution.py:161
  417.9 16.0 %fusion.5 = (bf16[128,6144]{1,0:T(8,128)(2,1)}, bf16[128,6144]{1,0:T(8,128)(2,1)}) fusion(bf16[128,6144]{1,0:T(8,128)(2,1)} %reduce-scatter.6.cloned.1.call-done, f32[6144]{0:T(1024)S(1)} %bitcast.55, bf16[128,6144]{1,0:T(8,128)(2,1)} %reduce-scatter.4.cloned.1.call-done), kind=kLoop, calls=%fused_computation.15 | loop fusion | flops 105381888 | bytes 6316032 | tf_op jit(solution)/shard_map/convert_element_type | solution.py:164
  433.9 0.0 all-gather.9.cloned.1.call-start
  434.0 0.5 all-gather.9.cloned.1.call-update
  434.5 0.3 reduce-scatter.8.cloned.1.call-start
  434.8 7.7 bitcast_select_fusion.1
  442.5 8.0 %pad_maximum_fusion = bf16[6144,1536]{1,0:T(8,128)(2,1)} fusion(bf16[6144,768]{1,0:T(8,128)(2,1)S(1)} %get-tuple-element.20, bf16[6144,768]{1,0:T(8,128)(2,1)S(1)} %get-tuple-element.19), kind=kLoop, calls=%fused_computation | loop fusion | flops 37748736 | bytes 37748736 | tf_op jit(solution)/shard_map/concatenate | solution.py:115
  450.5 99.4 %all-gather.11.cloned.1.call-done = bf16[512,6144]{1,0:T(8,128)(2,1)} async-done(((bf16[128,6144]{1,0:T(8,128)(2,1)}), bf16[512,6144]{1,0:T(8,128)(2,1)}) %all-gather.11.cloned.1.call-update) | async-done | bytes 6291472 | tf_op jit(solution)/shard_map/all_gather | solution.py:173
  549.9 15.6 %convolution_convert_fusion.2 = bf16[512,1536]{1,0:T(8,128)(2,1)S(1)} fusion(bf16[512,6144]{1,0:T(8,128)(2,1)} %all-gather.11.cloned.1.call-done, bf16[6144,1536]{1,0:T(8,128)(2,1)} %pad_maximum_fusion), kind=kOutput, calls=%fused_computation.58 | convolution fusion | flops 9664462848 | bytes 26738688 | tf_op jit(solution)/shard_map/dot_general | solution.py:172
  565.5 99.4 %all-gather.9.cloned.1.call-done = bf16[512,6144]{1,0:T(8,128)(2,1)} async-done(((bf16[128,6144]{1,0:T(8,128)(2,1)}), bf16[512,6144]{1,0:T(8,128)(2,1)}) %all-gather.9.cloned.1.call-update) | async-done | bytes 6291472 | tf_op jit(solution)/shard_map/all_gather | solution.py:173
  664.9 15.6 %convolution_convert_fusion.3 = bf16[512,1536]{1,0:T(8,128)(2,1)S(1)} fusion(bf16[512,6144]{1,0:T(8,128)(2,1)} %all-gather.9.cloned.1.call-done, bf16[6144,1536]{1,0:T(8,128)(2,1)} %pad_maximum_fusion), kind=kOutput, calls=%fused_computation.59 | convolution fusion | flops 9664462848 | bytes 26738688 | tf_op jit(solution)/shard_map/dot_general | solution.py:172
  680.5 1.8 pad_maximum_fusion.1
  682.3 0.0 all-reduce.4.cloned.1.call-start
  682.4 0.9 copy-done.5
  683.3 0.2 convolution_reduce_fusion
  683.5 40.6 %reduce-scatter.8.cloned.1.call-done = bf16[512,1536]{1,0:T(8,128)(2,1)} async-done(((bf16[1024,1536]{1,0:T(8,128)(2,1)}), bf16[512,1536]{1,0:T(8,128)(2,1)}) %reduce-scatter.8.cloned.1.call-update) | async-done | bytes 1572880 | tf_op jit(solution)/shard_map/reduce_scatter | solution.py:183
  724.1 3.2 fusion.32
  727.3 11.7 %all-reduce = (f32[512]{0:T(512)S(1)}, f32[512]{0:T(512)S(1)}) all-reduce(f32[512]{0:T(512)S(1)} %get-tuple-element.12, f32[512]{0:T(512)S(1)} %get-tuple-element.11), channel_id=1, replica_groups=mesh['rep'=4,'row'=4,'col'=2] {'row'}, use_global_device_ids=true, to_apply=%region_10.11 | all-reduce | flops 1024 | bytes 8192 | tf_op jit(solution)/shard_map/psum | solution.py:29
  739.0 3.6 fusion.26
  742.7 33.0 %all-reduce.4.cloned.1.call-done = f32[512,128]{1,0:T(8,128)} async-done(((f32[512,128]{1,0:T(8,128)}), f32[512,128]{1,0:T(8,128)}) %all-reduce.4.cloned.1.call-update) | async-done | bytes 262160 | tf_op jit(solution)/shard_map/psum | solution.py:187
  775.6 1.7 copy.22
  (28 shorter events, 0.2 us)
Async XLA Ops:
  7.2 58.7 %copy-start = (bf16[588,1536]{1,0:T(8,128)(2,1)S(1)}, bf16[588,1536]{1,0:T(8,128)(2,1)}, u32[]{:S(2)}) copy-start(bf16[588,1536]{1,0:T(8,128)(2,1)} %param.12) | copy-start | bytes 5419012
  7.2 126.7 %all-gather.5.cloned.1.call-start = ((), (), s32[]{:S(2)}) async-start(), calls=%async_computation.3 | async-start | bytes 11796480 | tf_op jit(solution)/shard_map/all_gather | solution.py:100
  10.6 54.5 %collective-permute-start = (bf16[768,1536]{1,0:T(8,128)(2,1)}, bf16[768,1536]{1,0:T(8,128)(2,1)}, u32[]{:S(2)}, u32[]{:S(2)}) collective-permute-start(bf16[768,1536]{1,0:T(8,128)(2,1)} %dynamic-slice_bitcast_fusion.2), channel_id=1, source_target_pairs={{0,1},{1,0},{2,3},{3,2},{4,5},{5,4},{6,7},{7,6},{8,9},{9,8},{10,11... | collective-permute-start | bytes 7077896 | tf_op jit(solution)/shard_map/ppermute | solution.py:17
  13.6 52.3 %copy-start.6 = (bf16[512,588]{0,1:T(8,128)(2,1)S(1)}, bf16[512,588]{0,1:T(8,128)(2,1)}, u32[]{:S(2)}) copy-start(bf16[512,588]{0,1:T(8,128)(2,1)} %param.11) | copy-start | bytes 1806340
  13.6 52.3 %copy-start.7 = (f32[1536]{0:T(1024)S(1)}, f32[1536]{0:T(1024)}, u32[]{:S(2)}) copy-start(f32[1536]{0:T(1024)} %param.13) | copy-start | bytes 18436
  65.1 112.4 %all-gather.7.cloned.1.call-start = ((), (), s32[]{:S(2)}) async-start(), calls=%async_computation.4 | async-start | bytes 4718592 | tf_op jit(solution)/shard_map/all_gather | solution.py:151
  65.9 15.5 %copy-start.4 = (f32[48,1536]{1,0:T(8,128)S(1)}, f32[48,1536]{1,0:T(8,128)}, u32[]{:S(2)}) copy-start(f32[48,1536]{1,0:T(8,128)} %param.17) | copy-start | bytes 884740
  85.2 219.2 %reduce-scatter.6.cloned.1.call-start = ((), (), s32[]{:S(2)}) async-start(), calls=%async_computation.7 | async-start | bytes 7864320 | tf_op jit(solution)/shard_map/reduce_scatter | solution.py:161
  193.5 224.4 %reduce-scatter.4.cloned.1.call-start = ((), (), s32[]{:S(2)}) async-start(), calls=%async_computation.5 | async-start | bytes 7864320 | tf_op jit(solution)/shard_map/reduce_scatter | solution.py:161
  209.7 1.3 copy-start.3
  209.7 340.2 %all-gather.11.cloned.1.call-start = ((), (), s32[]{:S(2)}) async-start(), calls=%async_computation.8 | async-start | bytes 7864320 | tf_op jit(solution)/shard_map/all_gather | solution.py:173
  211.5 222.5 %collective-permute-start.1 = (bf16[6144,768]{1,0:T(8,128)(2,1)}, bf16[6144,768]{1,0:T(8,128)(2,1)}, u32[]{:S(2)}, u32[]{:S(2)}) collective-permute-start(bf16[6144,768]{1,0:T(8,128)(2,1)} %dynamic-slice_bitcast_fusion), channel_id=1, source_target_pairs={{0,1},{1,0},{2,3},{3,2},{4,5},{5,4},{6,7},{7,6},{8,9},{9,8},{10,11... | collective-permute-start | bytes 28311560 | tf_op jit(solution)/shard_map/ppermute | solution.py:17
  433.9 231.0 %all-gather.9.cloned.1.call-start = ((), (), s32[]{:S(2)}) async-start(), calls=%async_computation.6 | async-start | bytes 7864320 | tf_op jit(solution)/shard_map/all_gather | solution.py:173
  434.5 289.6 %reduce-scatter.8.cloned.1.call-start = ((), (), s32[]{:S(2)}) async-start(), calls=%async_computation.9 | async-start | bytes 4718592 | tf_op jit(solution)/shard_map/reduce_scatter | solution.py:183
  682.3 1.0 copy-start.5
  682.3 56.7 %copy-start.8 = (f32[1536]{0:T(1024)S(1)}, f32[1536]{0:T(1024)}, u32[]{:S(2)}) copy-start(f32[1536]{0:T(1024)} %param.20) | copy-start | bytes 18436
  682.3 93.3 %all-reduce.4.cloned.1.call-start = ((), (), s32[]{:S(2)}) async-start(), calls=%async_computation.10 | async-start | bytes 524288 | tf_op jit(solution)/shard_map/psum | solution.py:187
  724.1 14.9 %copy-start.2 = (bf16[512,1536]{1,0:T(8,128)(2,1)S(1)}, bf16[512,1536]{1,0:T(8,128)(2,1)}, u32[]{:S(2)}) copy-start(bf16[512,1536]{1,0:T(8,128)(2,1)} %reduce-scatter.8.cloned.1.call-done) | copy-start | bytes 4718596
  739.0 38.3 %copy-start.1 = (bf16[588,1536]{1,0:T(8,128)(2,1)S(1)}, bf16[588,1536]{1,0:T(8,128)(2,1)}, u32[]{:S(2)}) copy-start(bf16[588,1536]{1,0:T(8,128)(2,1)} %param.12) | copy-start | bytes 5419012
Sparse Core Ops, SparseCore 0:
  65.3 65.7 all-gather.4
  132.6 44.8 all-gather.6
  193.6 110.7 reduce-scatter.5
  306.5 111.2 reduce-scatter.3
  434.1 115.8 all-gather.10
  551.3 113.5 all-gather.8
  682.4 41.6 reduce-scatter.7
  742.8 32.8 all-reduce.3
where the time goes:
time: 786 us; the launch traced here: 784 us
  waiting for transfers between devices  532 us (68%)
  local copies, waits for them, and re-layouts  97.8 us (12%)
  matrix products  70.9 us (9%)
  other arithmetic  40.4 us (5%)
  blocking collectives  23.9 us (3%)
  between operations  14.9 us (2%)
    reduce_scatter x2, waiting for transfers between devices, on_device(): lax.psum_scatter(partial_pre, 'row', scatter_dimension=0, tiled=True)  206 us
    all_gather x2, waiting for transfers between devices, on_device(): lax.all_gather(hidden, 'row', axis=0, tiled=True)  199 us
    ppermute x2, waiting for transfers between devices, partner(): return lax.ppermute(value, axis, pairs)  43.6 us
    reduce_scatter x1, waiting for transfers between devices, on_device(): lax.psum_scatter(partial_branch, 'col', scatter_dimension=0, tiled=True)  40.6 us
    transpose x3, local copies, waits for them, and re-layouts, as_rows(): return jnp.transpose(rows, (1, 0, 2)).reshape(1, tile_rows, half_cols)  33.5 us
    psum x1, waiting for transfers between devices, on_device(): lax.psum(jnp.dot(final_normed, check_weight, preferred_element_type=jnp.f...  33 us
    dot_general x2, matrix products, on_device(): jnp.dot(tokens[chunk * chunk_rows:(chunk + 1) * chunk_rows], in_weight, p...  32 us
    dot_general x2, matrix products, on_device(): jnp.dot(lax.all_gather(hidden, 'row', axis=0, tiled=True), out_weight, pr...  31.1 us
  transfers between devices with their start and end apart: 10, of which 8 were waited for; matrix products, arithmetic and copies ran while one was open for 21% of the time, Pallas kernels for 0%

commit v1 on v0

--- a/solution.py
+++ b/solution.py
@@ -1,6 +1,10 @@
+import functools
+
 import jax
 import jax.numpy as jnp
 from jax import lax
+from jax.experimental import pallas as pl
+from jax.experimental.pallas import tpu as pltpu
 from jax.sharding import PartitionSpec as P
 
 EPSILON = 1e-06
@@ -189,6 +193,265 @@
     )
     return (in_weight, out_weight, check_logits)
 
+TAIL_LOG2 = (
+    -0.9999999403953552,
+    -1.1511064767837524,
+    -0.4591980278491974,
+    -0.05252550542354584,
+    0.0070996368303895,
+    -0.00015319570957217366,
+    -0.00018990339594893157,
+    4.5312575821299106e-05,
+    -4.725873623101506e-06,
+    1.9546290275229694e-07,
+)
+TAIL_END = 6.0
+
+
+def exact_gelu(value):
+    size = jnp.abs(value)
+    at = jnp.minimum(size, TAIL_END)
+    power = TAIL_LOG2[-1]
+    for coefficient in TAIL_LOG2[-2::-1]:
+        power = power * at + coefficient
+    return jnp.maximum(value, 0.0) - size * jnp.exp2(power)
+
+
+def branch_kernel(blocks, tok_ref, scale_ref, map_ref, bias_ref, weight_ref, out_ref, total, held):
+    step = pl.program_id(0)
+
+    @pl.when(step == 0)
+    def _():
+        total[...] = jnp.zeros_like(total)
+        held[...] = jnp.zeros_like(held)
+
+    total[...] += jnp.dot(held[...], weight_ref[...], preferred_element_type=jnp.float32)
+    pre = jnp.dot(tok_ref[...], map_ref[0], preferred_element_type=jnp.float32)
+    held[...] = exact_gelu(pre * scale_ref[...] + bias_ref[...]).astype(held.dtype)
+
+    @pl.when(step == blocks)
+    def _():
+        out_ref[...] = total[...].astype(out_ref.dtype)
+
+
+def branch(tok, scale, maps, in_bias, out_weight, out_type, block):
+    rows, depth = tok.shape
+    groups, _, group_cols = maps.shape
+    hidden_count, features = out_weight.shape
+    blocks = hidden_count // block
+    per_group = group_cols // block
+
+    def now(step):
+        return jnp.minimum(step, blocks - 1)
+
+    def before(step):
+        return jnp.maximum(step - 1, 0)
+
+    return pl.pallas_call(
+        functools.partial(branch_kernel, blocks),
+        grid=(blocks + 1,),
+        out_shape=jax.ShapeDtypeStruct((rows, features), out_type),
+        in_specs=[
+            pl.BlockSpec((rows, depth), lambda i: (0, 0)),
+            pl.BlockSpec((rows, 1), lambda i: (0, 0)),
+            pl.BlockSpec((1, depth, block), lambda i: (now(i) // per_group, 0, now(i) % per_group)),
+            pl.BlockSpec((1, block), lambda i: (0, now(i))),
+            pl.BlockSpec((block, features), lambda i: (before(i), 0)),
+        ],
+        out_specs=pl.BlockSpec((rows, features), lambda i: (0, 0)),
+        scratch_shapes=[
+            pltpu.VMEM((rows, features), jnp.float32),
+            pltpu.VMEM((rows, block), jnp.bfloat16),
+        ],
+        compiler_params=pltpu.CompilerParams(vmem_limit_bytes=48 * 2**20),
+        cost_estimate=pl.CostEstimate(
+            flops=2 * rows * hidden_count * (depth + features),
+            bytes_accessed=2 * hidden_count * (depth + features),
+            transcendentals=rows * hidden_count,
+        ),
+        name="branch",
+    )(tok, scale, maps, in_bias[None, :], out_weight)
+
+
+def place_kernel(axis, count, place_ref, own_ref, *refs):
+    arrived, out_ref = refs[:-1], refs[-1]
+    col = place_ref[0]
+    extent = own_ref.shape[1 + axis]
+    step = pl.program_id(0)
+
+    def window(index):
+        start = pl.multiple_of(index * extent, 128)
+        return (pl.ds(start, extent), slice(None)) if axis == 0 else (slice(None), pl.ds(start, extent))
+
+    out_ref[window(col)] = own_ref[0]
+    for number in range(count):
+        @pl.when(step == number)
+        def _(number=number):
+            out_ref[window(1 - col)] = arrived[number][...]
+
+
+def place_tiles(old, arrived, axis):
+    count = len(arrived)
+    _, rows, cols = old.shape
+    place = jnp.stack([lax.axis_index("col"), lax.axis_index("rep")]).astype(jnp.int32)
+    if axis == 0:
+        out_shape, out_block = (2 * rows, count * cols), (2 * rows, cols)
+        out_map = lambda i, place: (0, place[1] ^ i)
+    else:
+        out_shape, out_block = (count * rows, 2 * cols), (rows, 2 * cols)
+        out_map = lambda i, place: (place[1] ^ i, 0)
+    return pl.pallas_call(
+        functools.partial(place_kernel, axis, count),
+        grid_spec=pltpu.PrefetchScalarGridSpec(
+            num_scalar_prefetch=1,
+            grid=(count,),
+            in_specs=[pl.BlockSpec((1, rows, cols), lambda i, place: (place[0] * count + (place[1] ^ i), 0, 0))]
+            + [pl.BlockSpec((rows, cols), lambda i, place: (0, 0))] * count,
+            out_specs=pl.BlockSpec(out_block, out_map),
+        ),
+        out_shape=jax.ShapeDtypeStruct(out_shape, old.dtype),
+        compiler_params=pltpu.CompilerParams(vmem_limit_bytes=56 * 2**20),
+        cost_estimate=pl.CostEstimate(
+            flops=2 * rows * cols * count * 4096, bytes_accessed=8 * rows * cols * count, transcendentals=0
+        ),
+        name="place",
+    )(place, old, *arrived)
+
+
+def rep_partner(value, mask):
+    return lax.ppermute(value, "rep", [(s, s ^ mask) for s in range(lax.axis_size("rep"))])
+
+
+def after(value, *others):
+    return lax.optimization_barrier((value,) + others)[0]
+
+
+def spread_over_rep(share, first):
+    across = rep_partner(share, 2)
+    return (share, rep_partner(share, 1), across, rep_partner(across, 1))
+
+
+def row_of(restore_id, table):
+    return lax.dynamic_slice_in_dim(table, restore_id[0], 1, axis=0)[0]
+
+
+def fast_device(
+    patches,
+    embed_weight,
+    embed_bias,
+    old_in,
+    old_out,
+    restore_id,
+    norm_gains,
+    in_biases,
+    out_biases,
+    final_gain,
+    check_weight,
+):
+    col, rep = lax.axis_index("col"), lax.axis_index("rep")
+    rep_count, row_count = lax.axis_size("rep"), lax.axis_size("row")
+    tile_rows = old_in.shape[1]
+    token_count, patch_size = patches.shape
+    feature_count = embed_weight.shape[1] * row_count
+    depth = -(-(patch_size + 1) // (32 * row_count)) * 32 * row_count
+
+    layer_gain = row_of(restore_id, norm_gains)
+    in_bias = row_of(restore_id, in_biases)
+    out_bias = row_of(restore_id, out_biases)
+
+    def tile(old, half):
+        return lax.dynamic_index_in_dim(old, half * rep_count + rep, 0, keepdims=False)
+
+    in_share = partner(tile(old_in, 1 - col), "col", 0)
+    embedded = jnp.dot(patches, embed_weight, preferred_element_type=jnp.float32) + embed_bias
+    weights32 = embed_weight.astype(jnp.float32)
+    check32 = check_weight.astype(jnp.float32) * final_gain[:, None]
+    sums = lax.psum(
+        (
+            jnp.sum(embedded, axis=1),
+            jnp.sum(embedded * embedded, axis=1),
+            jnp.sum(weights32, axis=1),
+            jnp.sum(embed_bias)[None],
+            jnp.sum(check32, axis=0),
+        ),
+        "row",
+    )
+    average = sums[0] / feature_count
+    scale = lax.rsqrt(sums[1] / feature_count - average * average + EPSILON)
+    weight_mean, bias_mean, check_sum = sums[2] / feature_count, sums[3] / feature_count, sums[4]
+
+    lifted = jnp.concatenate(
+        (
+            (weights32 - weight_mean[:, None]) * layer_gain,
+            ((embed_bias - bias_mean) * layer_gain)[None, :],
+            jnp.zeros((depth - patch_size - 1, embed_weight.shape[1]), jnp.float32),
+        ),
+        axis=0,
+    ).astype(jnp.bfloat16)
+    own_part = lax.dynamic_slice_in_dim(lifted, col * tile_rows, tile_rows, axis=1)
+    far_part = lax.dynamic_slice_in_dim(lifted, (1 - col) * tile_rows, tile_rows, axis=1)
+    near_map = jnp.dot(own_part, tile(old_in, col), preferred_element_type=jnp.float32)
+    far_map = jnp.dot(far_part, in_share, preferred_element_type=jnp.float32)
+    map_part = (near_map + far_map).astype(jnp.bfloat16)
+    map_piece = lax.psum_scatter(map_part, "row", scatter_dimension=0, tiled=True)
+    maps = lax.all_gather(map_piece, ("rep", "row"), axis=0, tiled=True)
+    maps = maps.reshape(rep_count, depth, old_in.shape[2])
+
+    tok = jnp.concatenate(
+        (
+            patches,
+            jnp.ones((token_count, 1), patches.dtype),
+            jnp.zeros((token_count, depth - patch_size - 1), patches.dtype),
+        ),
+        axis=1,
+    )
+    patches_sent, scale_sent = after((patches, scale), in_share)
+    far_patches = partner(patches_sent, "col", 0)
+    far_scale = partner(scale_sent, "col", 0)
+    far_tok = jnp.concatenate((far_patches, tok[:, patch_size:]), axis=1)
+
+    out_sent = after(tile(old_out, 1 - col), in_share, far_patches)
+    out_share = partner(out_sent, "col", 0)
+    out_weight = place_tiles(old_out, spread_over_rep(out_share, 2), 1)
+    in_sent = after(in_share, out_share)
+    in_weight = place_tiles(old_in, spread_over_rep(in_sent, 2), 0)
+
+    block = 512
+    far_total = branch(far_tok, far_scale[:, None], maps, in_bias, out_weight, jnp.bfloat16, block)
+    near_tok, far_total = lax.optimization_barrier((tok, far_total))
+    arrived = partner(far_total, "col", 0)
+    near_total = branch(near_tok, scale[:, None], maps, in_bias, out_weight, jnp.float32, block)
+    updated = embedded + near_total + arrived.astype(jnp.float32) + out_bias
+
+    def halves(value):
+        upper = lax.reduce_precision(value, 8, 7)
+        return upper.astype(jnp.bfloat16), (value - upper).astype(jnp.bfloat16)
+
+    updated_hi, updated_lo = halves(updated)
+    check_hi, check_lo = halves(check32)
+    raw = (
+        jnp.dot(updated_hi, check_hi, preferred_element_type=jnp.float32)
+        + jnp.dot(updated_lo, check_hi, preferred_element_type=jnp.float32)
+        + jnp.dot(updated_hi, check_lo, preferred_element_type=jnp.float32)
+    )
+    raw, total, squares = lax.psum(
+        (raw, jnp.sum(updated, axis=1), jnp.sum(updated * updated, axis=1)), "row"
+    )
+    average = (total / feature_count)[:, None]
+    spread = (squares / feature_count)[:, None] - average * average
+    check_logits = lax.rsqrt(spread + EPSILON) * (raw - average * check_sum)
+    return (in_weight, out_weight, check_logits)
+
+
+def on_either(*args):
+    old_in = args[3]
+    shared = (
+        lax.axis_size("col") == 2
+        and lax.axis_size("rep") == 4
+        and old_in.shape[0] == 2 * lax.axis_size("rep")
+    )
+    return fast_device(*args) if shared else on_device(*args)
+
 
 def solution(mesh):
     placed = (
@@ -205,7 +468,7 @@
         P("row", None),
     )
     return jax.shard_map(
-        on_device,
+        on_either,
         mesh=mesh,
         in_specs=placed,
         out_specs=(P("row", "col"), P("col", "row"), P(("rep", "col"), None)),

time: 786 us -> 371 us (0.47)
  waiting for transfers between devices: 532 us -> 196 us
  Pallas kernels: 0 us -> 90.4 us
  local copies, waits for them, and re-layouts: 97.8 us -> 7.9 us
  matrix products: 70.9 us -> 15.1 us
  other arithmetic: 40.4 us -> 8.15 us
  starting transfers between devices: 4.11 us -> 12.2 us
    all_gather x4 -> x1, waiting for transfers between devices: 208 us -> 0.01 us  [fast_device(): maps = lax.all_gather(map_piece, ('rep', 'row'), axis=0, tiled=True)]
    reduce_scatter x3 -> x1, waiting for transfers between devices: 247 us -> 43.2 us  [fast_device(): lax.psum_scatter(map_part, 'row', scatter_dimension=0, tiled=True)]
    pallas_call x0 -> x4, Pallas kernels: none -> 90.4 us  [the longest x2 62.4 us: branch(): pl.pallas_call(functools.partial(branch_kernel, blocks), grid=(blocks + 1...]
    dot_general x9 -> x6, matrix products: 70.9 us -> 15.1 us  [the longest x1 4.67 us: fast_device(): far_map = jnp.dot(far_part, in_share, preferred_element_type=jnp.float32)]
    ppermute x0 -> x6, waiting for transfers between devices: none -> 52.3 us  [rep_partner(): lax.ppermute(value, 'rep', [(s, s ^ mask) for s in range(lax.axis_size('r...]
    ppermute x2 -> x5, waiting for transfers between devices: 43.6 us -> 90.6 us  [partner(): return lax.ppermute(value, axis, pairs)]
    transpose x3 -> x0, local copies, waits for them, and re-layouts: 33.5 us -> none  [as_rows(): return jnp.transpose(rows, (1, 0, 2)).reshape(1, tile_rows, half_cols)]
    reshape x2 -> x0, local copies, waits for them, and re-layouts: 25.3 us -> none  [as_rows(): return jnp.transpose(rows, (1, 0, 2)).reshape(1, tile_rows, half_cols)]
  transfers between devices with their start and end apart: 10 -> 14, of which waited for: 8 -> 8; matrix products, arithmetic and copies ran while one was open for 21% -> 6% of each run, Pallas kernels for 0% -> 24%
where the time goes in v1:
time: 371 us; the launch traced here: 370 us
  waiting for transfers between devices  196 us (53%)
  Pallas kernels  90.4 us (24%)
  blocking collectives  24.5 us (7%)
  between operations  15.2 us (4%)
  matrix products  15.1 us (4%)
  starting transfers between devices  12.2 us (3%)
  other arithmetic  8.15 us (2%)
  local copies, waits for them, and re-layouts  7.9 us (2%)
    ppermute x5, waiting for transfers between devices, partner(): return lax.ppermute(value, axis, pairs)  90.6 us
    pallas_call x2, Pallas kernels, branch(): pl.pallas_call(functools.partial(branch_kernel, blocks), grid=(blocks + 1...  62.4 us
    ppermute x6, waiting for transfers between devices, rep_partner(): lax.ppermute(value, 'rep', [(s, s ^ mask) for s in range(lax.axis_size('r...  52.3 us
    reduce_scatter x1, waiting for transfers between devices, fast_device(): lax.psum_scatter(map_part, 'row', scatter_dimension=0, tiled=True)  43.2 us
    pallas_call x2, Pallas kernels, place_tiles(): pl.pallas_call(functools.partial(place_kernel, axis, count), grid_spec=pl...  28 us
    psum x2, blocking collectives, fast_device(): lax.psum((jnp.sum(embedded, axis=1), jnp.sum(embedded * embedded, axis=1)...  24.5 us
    psum x1, waiting for transfers between devices, fast_device(): lax.psum((raw, jnp.sum(updated, axis=1), jnp.sum(updated * updated, axis=...  10.1 us
    ppermute x5, starting transfers between devices, partner(): return lax.ppermute(value, axis, pairs)  8.97 us
  transfers between devices with their start and end apart: 14, of which 8 were waited for; matrix products, arithmetic and copies ran while one was open for 6% of the time, Pallas kernels for 24%

profile of v1, /device:TPU:0, one launch (start us, length us, event | category | flops | bytes accessed | tf_op | source)
XLA Modules:
  0.0 369.8 jit_solution(14797582967801042018)
XLA Ops:
  7.3 3.4 dynamic-slice_bitcast_fusion.1
  10.6 3.0 collective-permute-start
  14.3 0.6 reduce_sum.66
  14.9 0.3 convert_reduce_fusion
  15.2 4.3 %multiply_reduce_fusion.1 = (f32[512]{0:T(512)S(1)}, f32[512]{0:T(512)S(1)}, f32[512,1536]{1,0:T(8,128)}) fusion(f32[1536]{0:T(1024)S(1)} %copy-done.7, bf16[512,588]{0,1:T(8,128)(2,1)} %param.11, bf16[588,1536]{1,0:T(8,128)(2,1)S(1)} %copy-done.2), kind=kOutput, calls=%fused_computation.11 | convolution fusion | flops 927988736 | bytes 5564416 | tf_op jit(solution)/shard_map/dot_general | solution.py:366
  19.5 12.7 %all-reduce.2 = (f32[512]{0:T(512)S(1)}, f32[512]{0:T(512)S(1)}, f32[1]{0:T(128)}, f32[588]{0:T(1024)S(1)}) all-reduce(f32[512]{0:T(512)S(1)} %get-tuple-element.18, f32[512]{0:T(512)S(1)} %get-tuple-element.17, f32[1]{0:T(128)} %bitcast.6, f32[588]{0:T(1024)S(1)} %convert_reduce_fusion), channel_id=1, replica_groups=mesh['rep'=4,'row'=4,'col'=2] {'row'}, use_global_device_ids=true, to_apply=%region_3.4 | all-reduce | flops 1613 | bytes 12904 | tf_op jit(solution)/shard_map/psum | solution.py:369
  32.8 0.8 dynamic-slice_reduce_fusion.1
  33.7 0.1 pad.8.clone
  33.8 0.5 fusion.1
  34.3 0.4 maximum_maximum_fusion
  34.7 3.4 fusion.3
  38.0 27.1 %collective-permute-done.refs_0_ = bf16[768,1536]{1,0:T(8,128)(2,1)} collective-permute-done((bf16[768,1536]{1,0:T(8,128)(2,1)}, bf16[768,1536]{1,0:T(8,128)(2,1)}, u32[]{:S(2)}, u32[]{:S(2)}) %collective-permute-start) | collective-permute-done | bytes 2359328 | tf_op jit(solution)/shard_map/ppermute | solution.py:21
  65.2 4.7 %add_convert_fusion = bf16[640,1536]{1,0:T(8,128)(2,1)} fusion(f32[640,1536]{1,0:T(8,128)S(1)} %fusion.3, bf16[768,1536]{1,0:T(8,128)(2,1)} %collective-permute-done.refs_0_, bf16[640,1536]{1,0:T(8,128)(2,1)S(1)} %maximum_maximum_fusion, s32[]{:T(128)S(6)} %select_n.24), kind=kOutput, calls=%fused_computation.4 | convolution fusion | flops 1511915520 | bytes 9240580 | tf_op jit(solution)/shard_map/dot_general | solution.py:394
  69.9 0.0 all-gather.2.cloned.1.call-start
  69.9 43.2 %reduce-scatter.2.cloned.1.call-done = bf16[160,1536]{1,0:T(8,128)(2,1)} async-done(((bf16[640,1536]{1,0:T(8,128)(2,1)}), bf16[160,1536]{1,0:T(8,128)(2,1)}) %reduce-scatter.2.cloned.1.call-update) | async-done | bytes 491536 | tf_op jit(solution)/shard_map/reduce_scatter | solution.py:396
  113.1 0.2 all-reduce.5.cloned.1.call-start
  113.4 1.6 collective-permute-start.1
  114.9 1.8 dynamic-slice_bitcast_fusion
  116.7 11.7 %collective-permute-done.1 = bf16[512,588]{0,1:T(8,128)(2,1)S(1)} collective-permute-done((bf16[512,588]{0,1:T(8,128)(2,1)S(1)}, bf16[512,588]{0,1:T(8,128)(2,1)S(1)}, u32[]{:S(2)}, u32[]{:S(2)}) %collective-permute-start.1) | collective-permute-done | bytes 602144 | tf_op jit(solution)/shard_map/ppermute | solution.py:21
  128.5 1.5 collective-permute-start.2
  129.9 50.5 %collective-permute-done.2.refs_0_ = bf16[1536,768]{1,0:T(8,128)(2,1)} collective-permute-done((bf16[1536,768]{1,0:T(8,128)(2,1)S(1)}, bf16[1536,768]{1,0:T(8,128)(2,1)}, u32[]{:S(2)}, u32[]{:S(2)}) %collective-permute-start.2) | collective-permute-done | bytes 2359328 | tf_op jit(solution)/shard_map/ppermute | solution.py:21
  180.4 1.4 collective-permute-start.7
  181.9 49.9 %collective-permute-done.7.refs_2_ = bf16[1536,768]{1,0:T(8,128)(2,1)} collective-permute-done((bf16[1536,768]{1,0:T(8,128)(2,1)}, bf16[1536,768]{1,0:T(8,128)(2,1)}, u32[]{:S(2)}, u32[]{:S(2)}) %collective-permute-start.7) | collective-permute-done | bytes 2359328 | tf_op jit(solution)/shard_map/ppermute | solution.py:322
  231.8 1.5 collective-permute-start.9
  233.3 0.6 pad_add_fusion.place_ref
  233.9 0.3 copy.20
  234.2 1.3 collective-permute-done.9
  235.4 0.1 copy.22.scale_ref
  235.6 0.3 copy.21
  235.9 0.3 fusion.14
  236.2 1.5 collective-permute-start.4
  237.7 13.9 %place.3.weight_ref = bf16[6144,1536]{1,0:T(8,128)(2,1)} custom-call(s32[2]{0:T(128)} %pad_add_fusion.place_ref, bf16[8,1536,768]{2,1,0:T(8,128)(2,1)} %own_ref.3, bf16[1536,768]{1,0:T(8,128)(2,1)} %collective-permute-done.2.refs_0_, bf16[1536,768]{1,0:T(8,128)(2,1)} %collective-permute-done.6.refs_1_, bf16[1536,768]{1,0:T(8,128)(2,1)} %collective-permute-done.7.refs_2_, ...), custom_call_target="tpu_custom_call" | custom-call | flops 38654705664 | bytes 37748736 | tf_op jit(solution)/shard_map/place/pallas_call | solution.py:303
  251.6 31.2 %branch.2 = bf16[512,1536]{1,0:T(8,128)(2,1)S(1)} custom-call(bf16[512,640]{1,0:T(8,128)(2,1)S(1)} %get-tuple-element.27.tok_ref, f32[512,1]{1,0:T(8,128)S(1)} %copy.22.scale_ref, bf16[4,640,1536]{2,1,0:T(8,128)(2,1)} %bitcast.23, f32[1,6144]{1,0:T(1,128)S(1)} %constant_dynamic-slice_fusion.bias_ref, bf16[6144,1536]{1,0:T(8,128)(2,1)} %place.3.weight_ref), custom_call_target="tpu_custom_call" | custom-call | flops 13690208256 | bytes 26738688 | tf_op jit(solution)/shard_map/branch/pallas_call | solution.py:250
  282.8 1.5 collective-permute-start.10
  284.3 0.1 copy.23.scale_ref
  284.5 0.8 dynamic-slice_reduce_fusion
  285.3 1.3 fusion.13
  286.6 0.1 collective-permute-start.3
  286.7 2.4 collective-permute-done.4.refs_2_
  289.1 31.2 %branch.3 = f32[512,1536]{1,0:T(8,128)S(1)} custom-call(bf16[512,640]{1,0:T(8,128)(2,1)S(1)} %get-tuple-element.13.tok_ref, f32[512,1]{1,0:T(8,128)S(1)} %copy.23.scale_ref, bf16[4,640,1536]{2,1,0:T(8,128)(2,1)} %bitcast.24, f32[1,6144]{1,0:T(1,128)S(1)} %constant_dynamic-slice_fusion.bias_ref, bf16[6144,1536]{1,0:T(8,128)(2,1)} %place.3.weight_ref), custom_call_target="tpu_custom_call" | custom-call | flops 13690208256 | bytes 26738688 | tf_op jit(solution)/shard_map/branch/pallas_call | solution.py:250
  320.3 2.3 multiply_reduce_fusion
  322.6 0.7 fusion.15
  323.3 0.7 fusion.6
  324.0 1.4 fusion.9
  325.5 14.1 %place.2 = bf16[1536,6144]{1,0:T(8,128)(2,1)} custom-call(s32[2]{0:T(128)} %pad_add_fusion.place_ref, bf16[8,768,1536]{2,1,0:T(8,128)(2,1)} %own_ref.2, bf16[768,1536]{1,0:T(8,128)(2,1)} %collective-permute-done.refs_0_, bf16[768,1536]{1,0:T(8,128)(2,1)} %collective-permute-done.3.refs_1_, bf16[768,1536]{1,0:T(8,128)(2,1)} %collective-permute-done.4.refs_2_, ...), custom_call_target="tpu_custom_call" | custom-call | flops 38654705664 | bytes 37748736 | tf_op jit(solution)/shard_map/place/pallas_call | solution.py:303
  339.5 11.8 %all-reduce.1 = (f32[128]{0:T(128)S(1)}, f32[512]{0:T(512)S(1)}, f32[512]{0:T(512)S(1)}) all-reduce(f32[128]{0:T(128)S(1)} %fusion.13, f32[512]{0:T(512)S(1)} %get-tuple-element.16, f32[512]{0:T(512)S(1)} %get-tuple-element.15), channel_id=1, replica_groups=mesh['rep'=4,'row'=4,'col'=2] {'row'}, use_global_device_ids=true, to_apply=%region_15.16 | all-reduce | flops 1152 | bytes 9216 | tf_op jit(solution)/shard_map/psum | solution.py:369
  351.4 10.1 %all-reduce.5.cloned.1.call-done = f32[512,128]{1,0:T(8,128)} async-done(((f32[512,128]{1,0:T(8,128)}), f32[512,128]{1,0:T(8,128)}) %all-reduce.5.cloned.1.call-update) | async-done | bytes 262160 | tf_op jit(solution)/shard_map/psum | solution.py:437
  361.4 1.9 subtract_multiply_fusion
  (37 shorter events, 0.2 us)
Async XLA Ops:
  7.2 224.6 %copy-start = (f32[48,6144]{1,0:T(8,128)S(1)}, f32[48,6144]{1,0:T(8,128)}, u32[]{:S(2)}) copy-start(f32[48,6144]{1,0:T(8,128)} %param.18) | copy-start | bytes 3538948
  7.2 105.9 %reduce-scatter.2.cloned.1.call-start = ((), (), s32[]{:S(2)}) async-start(), calls=%async_computation.1 | async-start | bytes 2457600 | tf_op jit(solution)/shard_map/reduce_scatter | solution.py:396
  7.2 7.0 %copy-start.7 = (f32[1536]{0:T(1024)S(1)}, f32[1536]{0:T(1024)}, u32[]{:S(2)}) copy-start(f32[1536]{0:T(1024)} %param.13) | copy-start | bytes 18436
  7.2 7.7 %copy-start.2 = (bf16[588,1536]{1,0:T(8,128)(2,1)S(1)}, bf16[588,1536]{1,0:T(8,128)(2,1)}, u32[]{:S(2)}) copy-start(bf16[588,1536]{1,0:T(8,128)(2,1)} %param.12) | copy-start | bytes 5419012
  10.6 54.5 %collective-permute-start = (bf16[768,1536]{1,0:T(8,128)(2,1)}, bf16[768,1536]{1,0:T(8,128)(2,1)}, u32[]{:S(2)}, u32[]{:S(2)}) collective-permute-start(bf16[768,1536]{1,0:T(8,128)(2,1)} %dynamic-slice_bitcast_fusion.1), channel_id=1, source_target_pairs={{0,1},{1,0},{2,3},{3,2},{4,5},{5,4},{6,7},{7,6},{8,9},{9,8},{10,11... | collective-permute-start | bytes 7077896 | tf_op jit(solution)/shard_map/ppermute | solution.py:21
  69.8 43.5 %copy-start.5 = (bf16[512,588]{0,1:T(8,128)(2,1)S(1)}, bf16[512,588]{0,1:T(8,128)(2,1)}, u32[]{:S(2)}) copy-start(bf16[512,588]{0,1:T(8,128)(2,1)} %param.11) | copy-start | bytes 1806340
  69.9 181.7 %all-gather.2.cloned.1.call-start = ((), (), s32[]{:S(2)}) async-start(), calls=%async_computation.2 | async-start | bytes 8355840 | tf_op jit(solution)/shard_map/all_gather | solution.py:397
  113.1 248.3 %all-reduce.5.cloned.1.call-start = ((), (), s32[]{:S(2)}) async-start(), calls=%async_computation.3 | async-start | bytes 524288 | tf_op jit(solution)/shard_map/psum | solution.py:437
  113.4 15.1 %collective-permute-start.1 = (bf16[512,588]{0,1:T(8,128)(2,1)S(1)}, bf16[512,588]{0,1:T(8,128)(2,1)S(1)}, u32[]{:S(2)}, u32[]{:S(2)}) collective-permute-start(bf16[512,588]{0,1:T(8,128)(2,1)S(1)} %copy-done.5), channel_id=1, source_target_pairs={{0,1},{1,0},{2,3},{3,2},{4,5},{5,4},{6,7},{7,6},{8,9},{9,8},{10,11... | collective-permute-start | bytes 1806344 | tf_op jit(solution)/shard_map/ppermute | solution.py:21
  128.5 52.0 %collective-permute-start.2 = (bf16[1536,768]{1,0:T(8,128)(2,1)S(1)}, bf16[1536,768]{1,0:T(8,128)(2,1)}, u32[]{:S(2)}, u32[]{:S(2)}) collective-permute-start(bf16[1536,768]{1,0:T(8,128)(2,1)S(1)} %dynamic-slice_bitcast_fusion), channel_id=1, source_target_pairs={{0,1},{1,0},{2,3},{3,2},{4,5},{5,4},{6,7},{7,6},{8,9},{9,8},{10,11... | collective-permute-start | bytes 7077896 | tf_op jit(solution)/shard_map/ppermute | solution.py:21
  180.4 51.3 %collective-permute-start.7 = (bf16[1536,768]{1,0:T(8,128)(2,1)}, bf16[1536,768]{1,0:T(8,128)(2,1)}, u32[]{:S(2)}, u32[]{:S(2)}) collective-permute-start(bf16[1536,768]{1,0:T(8,128)(2,1)} %collective-permute-done.2.refs_0_), channel_id=1, source_target_pairs={{0,16},{8,24},{16,0},{24,8},{1,17},{9,25},{17,1},{25,9},{2,18},{10... | collective-permute-start | bytes 7077896 | tf_op jit(solution)/shard_map/ppermute | solution.py:322
  181.9 55.8 %collective-permute-start.6 = (bf16[1536,768]{1,0:T(8,128)(2,1)}, bf16[1536,768]{1,0:T(8,128)(2,1)}, u32[]{:S(2)}, u32[]{:S(2)}) collective-permute-start(bf16[1536,768]{1,0:T(8,128)(2,1)} %collective-permute-done.2.refs_0_), channel_id=1, source_target_pairs={{0,8},{8,0},{16,24},{24,16},{1,9},{9,1},{17,25},{25,17},{2,10},{10... | collective-permute-start | bytes 7077896 | tf_op jit(solution)/shard_map/ppermute | solution.py:322
  231.8 5.9 %collective-permute-start.8 = (bf16[1536,768]{1,0:T(8,128)(2,1)}, bf16[1536,768]{1,0:T(8,128)(2,1)}, u32[]{:S(2)}, u32[]{:S(2)}) collective-permute-start(bf16[1536,768]{1,0:T(8,128)(2,1)} %collective-permute-done.7.refs_2_), channel_id=1, source_target_pairs={{0,8},{8,0},{16,24},{24,16},{1,9},{9,1},{17,25},{25,17},{2,10},{10... | collective-permute-start | bytes 7077896 | tf_op jit(solution)/shard_map/ppermute | solution.py:322
  231.8 3.7 collective-permute-start.9
  236.2 52.9 %collective-permute-start.4 = (bf16[768,1536]{1,0:T(8,128)(2,1)}, bf16[768,1536]{1,0:T(8,128)(2,1)}, u32[]{:S(2)}, u32[]{:S(2)}) collective-permute-start(bf16[768,1536]{1,0:T(8,128)(2,1)} %collective-permute-done.refs_0_), channel_id=1, source_target_pairs={{0,16},{8,24},{16,0},{24,8},{1,17},{9,25},{17,1},{25,9},{2,18},{10... | collective-permute-start | bytes 7077896 | tf_op jit(solution)/shard_map/ppermute | solution.py:322
  251.6 33.7 %copy-start.6 = (f32[1536]{0:T(1024)S(1)}, f32[1536]{0:T(1024)}, u32[]{:S(2)}) copy-start(f32[1536]{0:T(1024)} %param.20) | copy-start | bytes 18436
  282.8 37.5 %collective-permute-start.10 = (bf16[512,1536]{1,0:T(8,128)(2,1)S(1)}, bf16[512,1536]{1,0:T(8,128)(2,1)}, u32[]{:S(2)}, u32[]{:S(2)}) collective-permute-start(bf16[512,1536]{1,0:T(8,128)(2,1)S(1)} %branch.2), channel_id=1, source_target_pairs={{0,1},{1,0},{2,3},{3,2},{4,5},{5,4},{6,7},{7,6},{8,9},{9,8},{10,11... | collective-permute-start | bytes 4718600 | tf_op jit(solution)/shard_map/ppermute | solution.py:21
  286.6 33.7 %copy-start.4 = (f32[512,1536]{1,0:T(8,128)S(1)}, f32[512,1536]{1,0:T(8,128)}, u32[]{:S(2)}) copy-start(f32[512,1536]{1,0:T(8,128)} %get-tuple-element.31) | copy-start | bytes 9437188
  286.6 38.8 %collective-permute-start.3 = (bf16[768,1536]{1,0:T(8,128)(2,1)}, bf16[768,1536]{1,0:T(8,128)(2,1)}, u32[]{:S(2)}, u32[]{:S(2)}) collective-permute-start(bf16[768,1536]{1,0:T(8,128)(2,1)} %collective-permute-done.refs_0_), channel_id=1, source_target_pairs={{0,8},{8,0},{16,24},{24,16},{1,9},{9,1},{17,25},{25,17},{2,10},{10... | collective-permute-start | bytes 7077896 | tf_op jit(solution)/shard_map/ppermute | solution.py:322
  289.1 36.4 %collective-permute-start.5 = (bf16[768,1536]{1,0:T(8,128)(2,1)}, bf16[768,1536]{1,0:T(8,128)(2,1)}, u32[]{:S(2)}, u32[]{:S(2)}) collective-permute-start(bf16[768,1536]{1,0:T(8,128)(2,1)} %collective-permute-done.4.refs_2_), channel_id=1, source_target_pairs={{0,8},{8,0},{16,24},{24,16},{1,9},{9,1},{17,25},{25,17},{2,10},{10... | collective-permute-start | bytes 7077896 | tf_op jit(solution)/shard_map/ppermute | solution.py:322
  320.3 2.3 copy-start.3
  325.5 37.8 %copy-start.1 = (f32[48,6144]{1,0:T(8,128)S(1)}, f32[48,6144]{1,0:T(8,128)}, u32[]{:S(2)}) copy-start(f32[48,6144]{1,0:T(8,128)} %param.18) | copy-start | bytes 3538948
Sparse Core Ops, SparseCore 0:
  70.0 43.0 reduce-scatter.1
  115.4 70.7 all-gather.1
  325.6 35.8 all-reduce.4

commit v2 on v0

--- a/solution.py
+++ b/solution.py
@@ -1,6 +1,10 @@
+import functools
+
 import jax
 import jax.numpy as jnp
 from jax import lax
+from jax.experimental import pallas as pl
+from jax.experimental.pallas import tpu as pltpu
 from jax.sharding import PartitionSpec as P
 
 EPSILON = 1e-06
@@ -190,6 +194,716 @@
     return (in_weight, out_weight, check_logits)
 
 
+TAIL_LOG2 = (
+    -0.9999999403953552,
+    -1.1511064767837524,
+    -0.4591980278491974,
+    -0.05252550542354584,
+    0.0070996368303895,
+    -0.00015319570957217366,
+    -0.00018990339594893157,
+    4.5312575821299106e-05,
+    -4.725873623101506e-06,
+    1.9546290275229694e-07,
+)
+TAIL_END = 6.0
+
+
+def exact_gelu(value):
+    size = jnp.abs(value)
+    at = jnp.minimum(size, TAIL_END)
+    power = TAIL_LOG2[-1]
+    for coefficient in TAIL_LOG2[-2::-1]:
+        power = power * at + coefficient
+    return jnp.maximum(value, 0.0) - size * jnp.exp2(power)
+
+
+def place_kernel(axis, place_ref, own_ref, early_ref, *refs):
+    late_refs, out_ref = refs[:-1], refs[-1]
+    col = place_ref[0]
+    step = pl.program_id(0)
+    rows, cols = own_ref.shape[1:]
+
+    def window(index):
+        start = pl.multiple_of(index * (rows, cols)[axis], 128)
+        return pl.ds(start, (rows, cols)[axis])
+
+    if axis == 1:
+        out_ref[:, window(col)] = own_ref[0]
+        out_ref[:, window(1 - col)] = early_ref[0]
+        return
+    out_ref[window(col)] = own_ref[0]
+    out_ref[window(1 - col), : cols // 2] = early_ref[0]
+    for number, late_ref in enumerate(late_refs):
+        @pl.when(step == number)
+        def _(late_ref=late_ref):
+            out_ref[window(1 - col), cols // 2 :] = late_ref[...]
+
+
+def place_tiles(old, arrived, axis, late=()):
+    count = arrived.shape[0]
+    _, rows, cols = old.shape
+    place = jnp.stack([lax.axis_index("col"), lax.axis_index("rep")]).astype(jnp.int32)
+    if axis == 0:
+        out_shape, out_block = (2 * rows, count * cols), (2 * rows, cols)
+        out_map = lambda i, place: (0, place[1] ^ i)
+    else:
+        out_shape, out_block = (count * rows, 2 * cols), (rows, 2 * cols)
+        out_map = lambda i, place: (place[1] ^ i, 0)
+    return pl.pallas_call(
+        functools.partial(place_kernel, axis),
+        grid_spec=pltpu.PrefetchScalarGridSpec(
+            num_scalar_prefetch=1,
+            grid=(count,),
+            in_specs=[
+                pl.BlockSpec((1, rows, cols), lambda i, place: (place[0] * count + (place[1] ^ i), 0, 0)),
+                pl.BlockSpec((1,) + arrived.shape[1:], lambda i, place: (place[1] ^ i, 0, 0)),
+            ]
+            + [pl.BlockSpec(piece.shape, lambda i, place: (0, 0)) for piece in late],
+            out_specs=pl.BlockSpec(out_block, out_map),
+        ),
+        out_shape=jax.ShapeDtypeStruct(out_shape, old.dtype),
+        compiler_params=pltpu.CompilerParams(vmem_limit_bytes=66_000_000),
+        cost_estimate=pl.CostEstimate(
+            flops=2 * rows * cols * count * 4096, bytes_accessed=8 * rows * cols * count, transcendentals=0
+        ),
+        name="place",
+    )(place, old, arrived, *late)
+
+
+MESH = pl.DeviceIdType.MESH
+STRIPS = 12
+PAIR = 2
+ROWS = 4
+PASSES = 6
+TICK_PASSES = (19,)
+
+
+def column(row, rows=128):
+    return jnp.transpose(jnp.broadcast_to(row, (rows, row.shape[1])))
+
+
+def gather_kernel(
+    patch_size, tok_ref, weight_ref, embed_bias_ref, gain_ref, bias_ref, old_in, old_out,
+    embedded_out, in_tiles, in_late, out_tiles, near_kept, near_late, far_got, late_got,
+    kept, far_sent, late_sent, sum_kept, sum_late, near, far, lifted, embedded, part, from_outer, from_inner, middle, final, maps, toks, scales, held,
+    sums, sums_in, stats, stats_in, scale_sent, scale_in,
+    near_sem, tile_sem, embed_sem, sums_sem, stats_sem, scale_sem, far_sem, tok_sem, outer_sem, middle_sem,
+    final_sem, keep_sem, across_sem, core_sem, relay_sem, out_sem, out_across_sem, out_core_sem, out_relay_sem,
+    kept_sem, got_sem, sum_sem, in_sem,
+):
+    rep, row, col = lax.axis_index("rep"), lax.axis_index("row"), lax.axis_index("col")
+    owners, strips, depth, width = maps.shape
+    half_rows = depth // 2
+    early = in_tiles.shape[2] // width
+    row_count = ROWS
+    out_rows = out_tiles.shape[1] // PASSES
+    features = weight_ref.shape[1] * row_count
+    side = row // 2
+    outer = (row == 0) | (row == 3)
+    inner = jnp.logical_not(outer)
+    own, other = side, 1 - side
+    outer_row, inner_row, other_inner = side * 3, 1 + side, 2 - side
+    far_col, far_rep, twin = {"col": 1 - col}, {"rep": rep ^ 2}, {"rep": rep ^ 1}
+    row_peers = [{"row": (row + step) % row_count} for step in range(1, row_count)]
+
+    barrier = pltpu.get_barrier_semaphore()
+    peers = [far_col, far_rep, twin] + row_peers
+    for device in peers:
+        pl.semaphore_signal(barrier, inc=1, device_id=device, device_id_type=MESH)
+    pl.semaphore_wait(barrier, len(peers))
+
+    def remote(source, target, sems, device):
+        return pltpu.make_async_remote_copy(
+            src_ref=source, dst_ref=target, send_sem=sems.at[0], recv_sem=sems.at[1],
+            device_id=device, device_id_type=MESH,
+        )
+
+    def columns(strip):
+        return pl.ds(pl.multiple_of(strip * width, width), width)
+
+    def half_block(half, strip):
+        return maps.at[rep, strip, pl.ds(pl.multiple_of(half * half_rows, 16), half_rows)]
+
+    def fetch_near(strip):
+        return pltpu.make_async_copy(
+            old_in.at[col * owners + rep, :, columns(strip)], near.at[strip], near_sem.at[strip]
+        )
+
+    def fetch_kept(owner):
+        return pltpu.make_async_copy(old_out.at[col * owners + owner], kept.at[owner], kept_sem.at[owner])
+
+    def fetch_late(owner):
+        return pltpu.make_async_copy(out_tiles.at[owner], kept.at[owner], kept_sem.at[owner])
+
+    def send_sum():
+        return remote(far_sent, far_got, got_sem.at[0], far_col)
+
+    def send_late():
+        return remote(late_sent, late_got, got_sem.at[1], far_col)
+
+    def keep_sum():
+        return pltpu.make_async_copy(sum_kept, near_kept, sum_sem.at[0])
+
+    def keep_late_sum():
+        return pltpu.make_async_copy(sum_late, near_late, sum_sem.at[1])
+
+    def send_far(strip):
+        source = old_in.at[(1 - col) * owners + rep, :, columns(strip)]
+        return remote(source, far.at[strip], far_sem.at[strip], far_col)
+
+    def keep_tile(strip):
+        return pltpu.make_async_copy(far.at[strip], in_tiles.at[rep, :, columns(strip)], tile_sem.at[strip])
+
+    def keep_late(strip):
+        return pltpu.make_async_copy(far.at[strip], in_late.at[:, columns(strip - early)], tile_sem.at[strip])
+
+    def in_across(strip):
+        return remote(far.at[strip], in_tiles.at[rep, :, columns(strip)], in_sem.at[strip, 0], far_rep)
+
+    def in_core(strip):
+        return remote(far.at[strip], in_tiles.at[rep, :, columns(strip)], in_sem.at[strip, 1], twin)
+
+    def in_relay(strip):
+        block = in_tiles.at[rep ^ 2, :, columns(strip)]
+        return remote(block, block, in_sem.at[strip, 2], twin)
+
+    def send_tok():
+        return remote(tok_ref, toks.at[1], tok_sem, far_col)
+
+    def send_sums(step):
+        return remote(sums, sums_in.at[step], sums_sem.at[step], row_peers[step])
+
+    def send_stats(step):
+        return remote(stats, stats_in.at[step], stats_sem.at[step], row_peers[step])
+
+    def send_scale():
+        return remote(scale_sent, scale_in, scale_sem, far_col)
+
+    def keep_embedded():
+        return pltpu.make_async_copy(embedded, embedded_out, embed_sem)
+
+    def out_block(owner, index):
+        return out_tiles.at[owner, pl.ds(index * out_rows, out_rows)]
+
+    def send_out(index):
+        source = old_out.at[(1 - col) * owners + rep, pl.ds(index * out_rows, out_rows)]
+        return remote(source, out_block(rep, index), out_sem.at[index], far_col)
+
+    def out_across(index):
+        return remote(out_block(rep, index), out_block(rep, index), out_across_sem.at[index], far_rep)
+
+    def out_core(index):
+        return remote(out_block(rep, index), out_block(rep, index), out_core_sem.at[index], twin)
+
+    def out_relay(index):
+        owner = rep ^ 2
+        return remote(out_block(owner, index), out_block(owner, index), out_relay_sem.at[index], twin)
+
+    def to_inner(strip, half, slot):
+        return remote(part.at[strip, half], from_outer.at[strip, slot], outer_sem.at[strip, slot], {"row": inner_row})
+
+    def to_middle(strip):
+        return remote(middle.at[strip], from_inner.at[strip], middle_sem.at[strip], {"row": other_inner})
+
+    def final_across(strip):
+        return remote(final.at[strip], half_block(own, strip), final_sem.at[strip, 0], {"row": other_inner})
+
+    def final_arrives(strip):
+        return remote(final.at[strip], half_block(other, strip), final_sem.at[strip, 0], {"row": other_inner})
+
+    def final_out(strip):
+        return remote(final.at[strip], half_block(own, strip), final_sem.at[strip, 1], {"row": outer_row})
+
+    def final_pass(strip):
+        return remote(half_block(other, strip), half_block(other, strip), final_sem.at[strip, 2], {"row": outer_row})
+
+    def final_keep(strip):
+        return pltpu.make_async_copy(final.at[strip], half_block(own, strip), keep_sem.at[strip])
+
+    def across(strip):
+        return remote(maps.at[rep, strip], maps.at[rep, strip], across_sem.at[strip], far_rep)
+
+    def to_core(strip):
+        return remote(maps.at[rep, strip], maps.at[rep, strip], core_sem.at[strip], twin)
+
+    def relay(strip):
+        return remote(maps.at[rep ^ 2, strip], maps.at[rep ^ 2, strip], relay_sem.at[strip], twin)
+
+    for strip in range(strips // 2):
+        send_far(strip).start()
+    for strip in range(strips):
+        fetch_near(strip).start()
+    for owner in range(owners):
+        fetch_kept(owner).start()
+
+    lane = lax.broadcasted_iota(jnp.int32, (8, depth), 1)
+    ones = jnp.ones((8, weight_ref.shape[1]), jnp.bfloat16)
+    weight_sums = lax.dot_general(
+        ones, weight_ref[...], (((1,), (1,)), ((), ())), preferred_element_type=jnp.float32
+    )
+    sums[...] = jnp.where(lane == patch_size, jnp.sum(embed_bias_ref[...]), weight_sums)
+    for step in range(row_count - 1):
+        send_sums(step).start()
+    toks[0] = tok_ref[...]
+    embedded[...] = (
+        jnp.dot(tok_ref[...], weight_ref[...], preferred_element_type=jnp.float32) + embed_bias_ref[...]
+    )
+    values = embedded[...]
+    lane = lax.broadcasted_iota(jnp.int32, (values.shape[0], 128), 1)
+    total = jnp.sum(values, axis=1, keepdims=True)
+    squares = jnp.sum(values * values, axis=1, keepdims=True)
+    stats[...] = jnp.transpose(jnp.where(lane == 0, total, squares))[:8]
+    for step in range(row_count - 1):
+        send_stats(step).start()
+    keep_embedded().start()
+
+    for step in range(row_count - 1):
+        send_sums(step).wait_recv()
+    mean = column((sums[...] + sums_in[0] + sums_in[1] + sums_in[2])[:1] / features)[:, :1]
+    extent = lifted.shape[2]
+    number = lax.broadcasted_iota(jnp.int32, (depth, extent), 0)
+    for half in range(2):
+        window = slice(half * extent, (half + 1) * extent)
+        raw = jnp.where(
+            number == patch_size, embed_bias_ref[:, window], weight_ref[:, window].astype(jnp.float32)
+        )
+        lifted[half] = ((raw - mean) * gain_ref[:, window]).astype(lifted.dtype)
+
+    for step in range(row_count - 1):
+        send_stats(step).wait_recv()
+    moments = (stats[...] + stats_in[0] + stats_in[1] + stats_in[2]) / features
+    spread = moments[1:2] - moments[:1] * moments[:1]
+    scale = lax.rsqrt(spread + EPSILON)
+    scale_sent[...] = jnp.broadcast_to(scale, scale_sent.shape)
+    send_scale().start()
+    for strip in range(strips // 2, strips):
+        send_far(strip).start()
+    send_tok().start()
+    for index in range(PASSES):
+        send_out(index).start()
+    scales[0] = column(scale)
+
+    def multiply(strip):
+        fetch_near(strip).wait()
+        send_far(strip).wait_recv()
+
+        @pl.when(strip < early)
+        def _():
+            keep_tile(strip).start()
+            in_across(strip).start()
+            in_core(strip).start()
+
+        @pl.when(strip >= early)
+        def _():
+            keep_late(strip).start()
+
+        total = jnp.dot(lifted[col], near[strip], preferred_element_type=jnp.float32) + jnp.dot(
+            lifted[1 - col], far[strip], preferred_element_type=jnp.float32
+        )
+        part[strip, 0] = total[:half_rows].astype(part.dtype)
+        part[strip, 1] = total[half_rows:].astype(part.dtype)
+
+        @pl.when(outer)
+        def _():
+            to_inner(strip, other, 0).start()
+            to_inner(strip, own, 1).start()
+
+    def halfway(strip):
+        @pl.when(inner)
+        def _():
+            to_inner(strip, other, 0).wait_recv()
+            middle[strip] = (
+                part[strip, other].astype(jnp.float32) + from_outer[strip, 0].astype(jnp.float32)
+            ).astype(middle.dtype)
+            to_middle(strip).start()
+
+    def finish(strip):
+        @pl.when(inner)
+        def _():
+            to_inner(strip, own, 1).wait_recv()
+            to_middle(strip).wait_recv()
+            final[strip] = (
+                part[strip, own].astype(jnp.float32)
+                + from_outer[strip, 1].astype(jnp.float32)
+                + from_inner[strip].astype(jnp.float32)
+            ).astype(final.dtype)
+            final_across(strip).start()
+            final_out(strip).start()
+            final_keep(strip).start()
+
+    def settle(strip):
+        @pl.when(inner)
+        def _():
+            final_arrives(strip).wait_recv()
+            final_pass(strip).start()
+            final_keep(strip).wait()
+            across(strip).start()
+            to_core(strip).start()
+
+    def settle_outer(strip):
+        @pl.when(outer)
+        def _():
+            final_out(strip).wait_recv()
+            final_pass(strip).wait_recv()
+            across(strip).start()
+            to_core(strip).start()
+
+    def hand_on(strip):
+        across(strip).wait_recv()
+        relay(strip).start()
+
+        @pl.when(strip < early)
+        def _():
+            in_across(strip).wait_recv()
+            in_relay(strip).start()
+
+    block = PAIR * width
+    blocks = strips // PAIR
+
+    def owner_of(turn):
+        return rep ^ (turn % 2 * 2 + turn // 2)
+
+    def activate(pair, turn, half):
+        owner = owner_of(turn)
+        unit = (pair * owners + turn) * 2 + half
+        applied = jnp.concatenate([maps[owner, pair * PAIR + number] for number in range(PAIR)], axis=1)
+        pre = jnp.dot(toks[half], applied, preferred_element_type=jnp.float32)
+        scale = jnp.concatenate([scales[half]] * (block // 128), axis=1)
+        held[unit] = exact_gelu(pre * scale + bias_ref[owner * blocks + pair]).astype(held.dtype)
+
+    def activate_near(strip):
+        @pl.when(strip % PAIR == PAIR - 1)
+        def _():
+            pair = strip // PAIR
+
+            def piece(turn, carry):
+                @pl.when(turn == 2)
+                def _():
+                    for number in range(PAIR):
+                        to_core(pair * PAIR + number).wait_recv()
+
+                @pl.when(turn == 3)
+                def _():
+                    for number in range(PAIR):
+                        relay(pair * PAIR + number).wait_recv()
+
+                activate(pair, turn, 0)
+                return carry
+
+            lax.fori_loop(0, owners, piece, 0)
+
+    def pass_out(index):
+        if index < PASSES:
+            send_out(index).wait_recv()
+            out_across(index).start()
+            out_core(index).start()
+        if index:
+            out_across(index - 1).wait_recv()
+            out_relay(index - 1).start()
+
+    stages = (
+        (0, multiply), (1, halfway), (2, finish), (3, settle), (5, settle_outer), (7, hand_on), (9, activate_near)
+    )
+
+    def advance(tick, carry):
+        for delay, stage in stages:
+            strip = tick - delay
+
+            @pl.when((strip >= 0) & (strip < strips))
+            def _(stage=stage, strip=strip):
+                stage(strip)
+
+        for index, moment in enumerate(TICK_PASSES):
+            @pl.when(tick == moment)
+            def _(index=index):
+                pass_out(index)
+
+        return carry
+
+    def with_passes(count, first, moments, work):
+        def step(number, carry):
+            work(number)
+            for index, moment in enumerate(moments):
+                @pl.when(number == moment)
+                def _(index=index):
+                    pass_out(first + index)
+
+            return carry
+
+        lax.fori_loop(0, count, step, 0)
+
+    lax.fori_loop(0, strips + stages[-1][0], advance, 0)
+    send_tok().wait_recv()
+    send_scale().wait_recv()
+    scales[1] = column(scale_in[:1])
+    pieces = blocks * owners
+    with_passes(
+        pieces, 1, (pieces // 4, 2 * pieces // 3, pieces - 1),
+        lambda number: activate(number // owners, number % owners, 1),
+    )
+    for owner in range(owners):
+        fetch_kept(owner).wait()
+
+    def add_up(half, total):
+        def step(turn):
+            rows = [held[(pair * owners + turn) * 2 + half] for pair in range(blocks)]
+            total[...] += jnp.dot(
+                jnp.concatenate(rows, axis=1), kept[owner_of(turn)], preferred_element_type=jnp.float32
+            )
+
+        return step
+
+    sum_kept[...] = jnp.zeros_like(sum_kept)
+    with_passes(owners, 4, (owners - 1,), add_up(1, sum_kept))
+    far_sent[...] = sum_kept[...].astype(far_sent.dtype)
+    send_sum().start()
+    sum_kept[...] = jnp.zeros_like(sum_kept)
+    with_passes(owners, 5, (0,), add_up(0, sum_kept))
+    keep_sum().start()
+
+    fetch_late(rep).start()
+    pass_out(PASSES)
+    for index in range(PASSES):
+        out_core(index).wait_recv()
+    for turn in (1, 2):
+        fetch_late(owner_of(turn)).start()
+    for index in range(PASSES):
+        out_relay(index).wait_recv()
+    fetch_late(owner_of(owners - 1)).start()
+    for owner in range(owners):
+        fetch_late(owner).wait()
+    sum_late[...] = jnp.zeros_like(sum_late)
+    with_passes(owners, 0, (), add_up(1, sum_late))
+    late_sent[...] = sum_late[...].astype(late_sent.dtype)
+    send_late().start()
+    sum_late[...] = jnp.zeros_like(sum_late)
+    with_passes(owners, 0, (), add_up(0, sum_late))
+    keep_late_sum().start()
+
+    def finish_strip(strip, carry):
+        for copy in (across(strip), to_core(strip), relay(strip), send_far(strip)):
+            copy.wait_send()
+
+        @pl.when(strip < early)
+        def _():
+            keep_tile(strip).wait()
+            in_core(strip).wait()
+            in_relay(strip).wait()
+            in_across(strip).wait_send()
+
+        @pl.when(strip >= early)
+        def _():
+            keep_late(strip).wait()
+
+        @pl.when(outer)
+        def _():
+            to_inner(strip, other, 0).wait_send()
+            to_inner(strip, own, 1).wait_send()
+
+        @pl.when(inner)
+        def _():
+            for copy in (to_middle(strip), final_across(strip), final_out(strip), final_pass(strip)):
+                copy.wait_send()
+
+        return carry
+
+    lax.fori_loop(0, strips, finish_strip, 0)
+
+    keep_sum().wait()
+    keep_late_sum().wait()
+    for step in range(row_count - 1):
+        send_sums(step).wait_send()
+        send_stats(step).wait_send()
+    keep_embedded().wait()
+    for copy in (send_scale(), send_tok()):
+        copy.wait_send()
+    for index in range(PASSES):
+        for copy in (send_out(index), out_across(index), out_core(index), out_relay(index)):
+            copy.wait_send()
+    send_sum().wait()
+    send_late().wait()
+
+
+def gather_hidden(patch_size, tok, weight, embed_bias, gain, in_bias, old_in, old_out):
+    rep_count = lax.axis_size("rep")
+    tokens, depth = tok.shape
+    local = weight.shape[1]
+    _, tile_rows, group_cols = old_in.shape
+    width, half_rows = group_cols // STRIPS, depth // 2
+    any_space = pl.BlockSpec(memory_space=pl.ANY)
+    vmem = pl.BlockSpec(memory_space=pltpu.VMEM)
+    strip_shape = (half_rows, width)
+    units = 2 * rep_count * STRIPS // PAIR
+    dma = pltpu.SemaphoreType.DMA
+    f32, bf16 = jnp.float32, jnp.bfloat16
+    return pl.pallas_call(
+        functools.partial(gather_kernel, patch_size),
+        out_shape=(
+            jax.ShapeDtypeStruct((tokens, local), f32),
+            jax.ShapeDtypeStruct((rep_count, tile_rows, group_cols // 2), old_in.dtype),
+            jax.ShapeDtypeStruct((tile_rows, group_cols // 2), old_in.dtype),
+            jax.ShapeDtypeStruct((rep_count,) + old_out.shape[1:], old_out.dtype),
+            jax.ShapeDtypeStruct((tokens, tile_rows), f32),
+            jax.ShapeDtypeStruct((tokens, tile_rows), f32),
+            jax.ShapeDtypeStruct((tokens, tile_rows), bf16),
+            jax.ShapeDtypeStruct((tokens, tile_rows), bf16),
+        ),
+        in_specs=[vmem] * 5 + [any_space] * 2,
+        out_specs=(any_space,) * 8,
+        scratch_shapes=[
+            pltpu.VMEM((rep_count,) + old_out.shape[1:], old_out.dtype),
+            pltpu.VMEM((tokens, tile_rows), bf16),
+            pltpu.VMEM((tokens, tile_rows), bf16),
+            pltpu.VMEM((tokens, tile_rows), f32),
+            pltpu.VMEM((tokens, tile_rows), f32),
+            pltpu.VMEM((STRIPS, tile_rows, width), old_in.dtype),
+            pltpu.VMEM((STRIPS, tile_rows, width), old_in.dtype),
+            pltpu.VMEM((2, depth, tile_rows), bf16),
+            pltpu.VMEM((tokens, local), f32),
+            pltpu.VMEM((STRIPS, 2) + strip_shape, bf16),
+            pltpu.VMEM((STRIPS, 2) + strip_shape, bf16),
+            pltpu.VMEM((STRIPS,) + strip_shape, bf16),
+            pltpu.VMEM((STRIPS,) + strip_shape, bf16),
+            pltpu.VMEM((STRIPS,) + strip_shape, bf16),
+            pltpu.VMEM((rep_count, STRIPS, depth, width), bf16),
+            pltpu.VMEM((2, tokens, depth), bf16),
+            pltpu.VMEM((2, tokens, 128), f32),
+            pltpu.VMEM((units, tokens, PAIR * width), bf16),
+            pltpu.VMEM((8, depth), f32),
+            pltpu.VMEM((ROWS - 1, 8, depth), f32),
+            pltpu.VMEM((8, tokens), f32),
+            pltpu.VMEM((ROWS - 1, 8, tokens), f32),
+            pltpu.VMEM((8, tokens), f32),
+            pltpu.VMEM((8, tokens), f32),
+            dma((STRIPS,)),
+            dma((STRIPS,)),
+            dma,
+            dma((ROWS - 1, 2)),
+            dma((ROWS - 1, 2)),
+            dma((2,)),
+            dma((STRIPS, 2)),
+            dma((2,)),
+            dma((STRIPS, 2, 2)),
+            dma((STRIPS, 2)),
+            dma((STRIPS, 3, 2)),
+            dma((STRIPS,)),
+            dma((STRIPS, 2)),
+            dma((STRIPS, 2)),
+            dma((STRIPS, 2)),
+            dma((PASSES, 2)),
+            dma((PASSES, 2)),
+            dma((PASSES, 2)),
+            dma((PASSES, 2)),
+            dma((rep_count,)),
+            dma((2, 2)),
+            dma((2,)),
+            dma((STRIPS // 2, 3, 2)),
+        ],
+        compiler_params=pltpu.CompilerParams(
+            collective_id=0, has_side_effects=True, vmem_limit_bytes=66_000_000
+        ),
+        cost_estimate=pl.CostEstimate(flops=10**10, bytes_accessed=10**8, transcendentals=0),
+        name="gather_hidden",
+    )(tok, weight, embed_bias[None], gain[None], in_bias.reshape(-1, 1, PAIR * width), old_in, old_out)
+
+
+def rep_partner(value, mask):
+    return lax.ppermute(value, "rep", [(s, s ^ mask) for s in range(lax.axis_size("rep"))])
+
+
+def after(value, *others):
+    return lax.optimization_barrier((value,) + others)[0]
+
+
+def row_of(restore_id, table):
+    return lax.dynamic_slice_in_dim(table, restore_id[0], 1, axis=0)[0]
+
+
+def fast_device(
+    patches,
+    embed_weight,
+    embed_bias,
+    old_in,
+    old_out,
+    restore_id,
+    norm_gains,
+    in_biases,
+    out_biases,
+    final_gain,
+    check_weight,
+):
+    col = lax.axis_index("col")
+    row_count = lax.axis_size("row")
+    token_count, patch_size = patches.shape
+    feature_count = embed_weight.shape[1] * row_count
+    depth = -(-(patch_size + 1) // 32) * 32
+
+    layer_gain = row_of(restore_id, norm_gains)
+    in_bias = row_of(restore_id, in_biases)
+    out_bias = row_of(restore_id, out_biases)
+
+    check32 = check_weight.astype(jnp.float32) * final_gain[:, None]
+    tok = jnp.concatenate(
+        (
+            patches,
+            jnp.ones((token_count, 1), patches.dtype),
+            jnp.zeros((token_count, depth - patch_size - 1), patches.dtype),
+        ),
+        axis=1,
+    )
+    weight = jnp.pad(embed_weight, ((0, depth - patch_size), (0, 0)))
+    embedded, in_tiles, in_late, out_tiles, near_kept, near_late, far_got, late_got = gather_hidden(
+        patch_size, tok, weight, embed_bias, layer_gain, in_bias, old_in, old_out
+    )
+    late_across = rep_partner(in_late, 2)
+    late_core = rep_partner(in_late, 1)
+    branch_parts = (
+        near_kept + late_got.astype(jnp.float32),
+        near_late + far_got.astype(jnp.float32),
+    )
+    branch = jnp.where(
+        col == 0, jnp.concatenate(branch_parts, axis=1), jnp.concatenate(branch_parts[::-1], axis=1)
+    )
+    updated = embedded + branch + out_bias
+
+    def halves(value):
+        upper = lax.reduce_precision(value, 8, 7)
+        return upper.astype(jnp.bfloat16), (value - upper).astype(jnp.bfloat16)
+
+    updated_hi, updated_lo = halves(updated)
+    check_hi, check_lo = halves(check32)
+    raw = (
+        jnp.dot(updated_hi, check_hi, preferred_element_type=jnp.float32)
+        + jnp.dot(updated_lo, check_hi, preferred_element_type=jnp.float32)
+        + jnp.dot(updated_hi, check_lo, preferred_element_type=jnp.float32)
+    )
+    shares = (raw, jnp.sum(updated, axis=1), jnp.sum(updated * updated, axis=1))
+    out_tiles = after(out_tiles, *shares)
+    raw = lax.psum(shares[0], "row")
+    total, squares = lax.psum(shares[1:], "row")
+    check_sum = lax.psum(jnp.sum(check32, axis=0), "row")
+    out_weight = place_tiles(old_out, out_tiles, 1)
+    late_relay = rep_partner(after(late_across, out_weight), 1)
+    in_weight = place_tiles(old_in, in_tiles, 0, (in_late, late_core, late_across, late_relay))
+    raw, in_weight, out_weight = lax.optimization_barrier((raw, in_weight, out_weight))
+    average = (total / feature_count)[:, None]
+    spread = (squares / feature_count)[:, None] - average * average
+    check_logits = lax.rsqrt(spread + EPSILON) * (raw - average * check_sum)
+    return (in_weight, out_weight, check_logits)
+
+
+def on_either(*args):
+    old_in = args[3]
+    shared = (
+        lax.axis_size("col") == 2
+        and lax.axis_size("rep") == 4
+        and lax.axis_size("row") == ROWS
+        and old_in.shape[0] == 2 * lax.axis_size("rep")
+    )
+    return fast_device(*args) if shared else on_device(*args)
+
+
 def solution(mesh):
     placed = (
         P(("rep", "col"), None),
@@ -205,7 +919,7 @@
         P("row", None),
     )
     return jax.shard_map(
-        on_device,
+        on_either,
         mesh=mesh,
         in_specs=placed,
         out_specs=(P("row", "col"), P("col", "row"), P(("rep", "col"), None)),

time: 786 us -> 257 us (0.33)
  waiting for transfers between devices: 532 us -> 14.8 us
  Pallas kernels: 0 us -> 195 us
  local copies, waits for them, and re-layouts: 97.8 us -> 10.3 us
  matrix products: 70.9 us -> 2.78 us
  other arithmetic: 40.4 us -> 6.53 us
  blocking collectives: 23.9 us -> 10.4 us
    reduce_scatter x3 -> x0, waiting for transfers between devices: 247 us -> none  [the longest x2 206 us: on_device(): lax.psum_scatter(partial_pre, 'row', scatter_dimension=0, tiled=True)]
    all_gather x4 -> x0, waiting for transfers between devices: 208 us -> none  [the longest x2 199 us: on_device(): lax.all_gather(hidden, 'row', axis=0, tiled=True)]
    pallas_call x0 -> x3, Pallas kernels: none -> 195 us  [the longest x1 167 us: gather_hidden(): pl.pallas_call(functools.partial(gather_kernel, patch_size), out_shape=(j...]
    dot_general x9 -> x3, matrix products: 70.9 us -> 2.78 us  [the longest x1 1.41 us: fast_device(): jnp.dot(updated_lo, check_hi, preferred_element_type=jnp.float32)]
    ppermute x2 -> x3, waiting for transfers between devices: 43.6 us -> 5.21 us  [rep_partner(): lax.ppermute(value, 'rep', [(s, s ^ mask) for s in range(lax.axis_size('r...]
    transpose x3 -> x0, local copies, waits for them, and re-layouts: 33.5 us -> none  [as_rows(): return jnp.transpose(rows, (1, 0, 2)).reshape(1, tile_rows, half_cols)]
    reshape x2 -> x0, local copies, waits for them, and re-layouts: 25.3 us -> none  [as_rows(): return jnp.transpose(rows, (1, 0, 2)).reshape(1, tile_rows, half_cols)]
    psum x1, waiting for transfers between devices: 33 us -> 9.53 us  [fast_device(): raw = lax.psum(shares[0], 'row')]
  transfers between devices with their start and end apart: 10 -> 4, of which waited for: 8 -> 2; matrix products, arithmetic and copies ran while one was open for 21% -> 3% of each run, Pallas kernels for 0% -> 11%
where the time goes in v2:
time: 257 us; the launch traced here: 256 us
  Pallas kernels  195 us (76%)
  waiting for transfers between devices  14.8 us (6%)
  between operations  14.8 us (6%)
  blocking collectives  10.4 us (4%)
  local copies, waits for them, and re-layouts  10.3 us (4%)
  other arithmetic  6.53 us (3%)
  matrix products  2.78 us (1%)
    pallas_call x1, Pallas kernels, gather_hidden(): pl.pallas_call(functools.partial(gather_kernel, patch_size), out_shape=(j...  167 us
    pallas_call x2, Pallas kernels, place_tiles(): pl.pallas_call(functools.partial(place_kernel, axis), grid_spec=pltpu.Pre...  27.5 us
    psum x1, blocking collectives, fast_device(): check_sum = lax.psum(jnp.sum(check32, axis=0), 'row')  10.4 us
    psum x1, waiting for transfers between devices, fast_device(): raw = lax.psum(shares[0], 'row')  9.53 us
    ppermute x3, waiting for transfers between devices, rep_partner(): lax.ppermute(value, 'rep', [(s, s ^ mask) for s in range(lax.axis_size('r...  5.21 us
  transfers between devices with their start and end apart: 4, of which 2 were waited for; matrix products, arithmetic and copies ran while one was open for 3% of the time, Pallas kernels for 11%

profile of v2, /device:TPU:0, one launch (start us, length us, event | category | flops | bytes accessed | tf_op | source)
XLA Modules:
  0.0 256.2 jit_solution(2948847281337741175)
XLA Ops:
  7.2 0.0 all-reduce.4.cloned.1.call-start
  7.2 1.4 copy.14
  8.6 0.0 copy-start.5
  8.6 0.1 pad.13.clone
  8.7 0.1 pad.12.clone
  8.8 2.9 %pad.4.weight_ref = bf16[608,1536]{1,0:T(8,128)(2,1)} pad(bf16[588,1536]{1,0:T(8,128)(2,1)} %param.12, bf16[]{:T(256)} %constant.10.clone.1), padding=0_20x0_0 | pad | bytes 3674114 | tf_op jit(solution)/shard_map/jit(_pad)/pad | solution.py:855
  11.6 0.0 copy-done.5
  11.6 0.6 broadcast_in_dim.15.embed_bias_ref
  12.9 1.6 constant_dynamic-slice_fusion
  14.4 1.4 dynamic-slice_reduce_fusion
  15.8 1.0 maximum_maximum_fusion.tok_ref
  16.8 167.4 %gather_hidden.1 = (f32[512,1536]{1,0:T(8,128)}, bf16[4,768,768]{2,1,0:T(8,128)(2,1)}, bf16[768,768]{1,0:T(8,128)(2,1)}, bf16[4,1536,768]{2,1,0:T(8,128)(2,1)}, ...) custom-call(bf16[512,608]{1,0:T(8,128)(2,1)} %maximum_maximum_fusion.tok_ref, ...), custom_call_target="tpu_custom_call" | custom-call | flops 10000000000 | bytes 100000000 | tf_op jit(solution)/shard_map/gather_hidden/pallas_call | solution.py:740
  184.2 0.1 collective-permute-start
  184.3 1.6 collective-permute-start.1
  185.9 0.0 copy-start.2
  185.9 0.0 copy-start.3
  185.9 1.9 convert_add_fusion.1
  187.8 0.2 copy-done.2
  188.0 0.2 copy-done.3
  188.2 0.0 copy-start.1
  188.2 0.1 convert_add_fusion
  188.4 1.7 copy-done.1
  190.1 0.0 copy-start
  190.1 0.0 copy-start.4
  190.1 0.7 multiply_reduce_fusion
  190.9 0.2 copy-done
  191.1 0.0 copy-done.4
  191.1 0.7 fusion.13
  191.8 0.7 fusion.14
  192.5 1.4 fusion.8
  193.9 0.6 pad_add_fusion.place_ref
  194.5 13.3 %place.2 = bf16[6144,1536]{1,0:T(8,128)(2,1)} custom-call(s32[2]{0:T(128)} %pad_add_fusion.place_ref, bf16[8,1536,768]{2,1,0:T(8,128)(2,1)} %own_ref.2, bf16[4,1536,768]{2,1,0:T(8,128)(2,1)} %get-tuple-element.24.early_ref), custom_call_target="tpu_custom_call" | custom-call | flops 38654705664 | bytes 37748736 | tf_op jit(solution)/shard_map/place/pallas_call | solution.py:253
  207.8 5.2 %collective-permute-done.1.refs_2_ = bf16[768,768]{1,0:T(8,128)(2,1)} collective-permute-done((bf16[768,768]{1,0:T(8,128)(2,1)}, bf16[768,768]{1,0:T(8,128)(2,1)}, u32[]{:S(2)}, u32[]{:S(2)}) %collective-permute-start.1) | collective-permute-done | bytes 1179680 | tf_op jit(solution)/shard_map/ppermute | solution.py:812
  213.0 0.0 collective-permute-start.2
  213.0 0.0 all-reduce.4.cloned.1.call-update
  213.0 0.3 fusion.12
  213.3 10.4 %all-reduce.1 = (f32[128]{0:T(128)S(1)}, f32[512]{0:T(512)S(1)}, f32[512]{0:T(512)S(1)}) all-reduce(f32[128]{0:T(128)S(1)} %fusion.12, f32[512]{0:T(512)S(1)} %get-tuple-element.30, f32[512]{0:T(512)S(1)} %get-tuple-element.29), channel_id=1, replica_groups=mesh['rep'=4,'row'=4,'col'=2] {'row'}, use_global_device_ids=true, to_apply=%region_6.7 | all-reduce | flops 1152 | bytes 9216 | tf_op jit(solution)/shard_map/psum | solution.py:885
  223.8 0.0 collective-permute-done.refs_1_
  223.8 0.0 collective-permute-done.2.refs_3_
  223.8 14.2 %place.3 = bf16[1536,6144]{1,0:T(8,128)(2,1)} custom-call(s32[2]{0:T(128)} %pad_add_fusion.place_ref, bf16[8,768,1536]{2,1,0:T(8,128)(2,1)} %own_ref.3, bf16[4,768,768]{2,1,0:T(8,128)(2,1)} %get-tuple-element.21.early_ref, bf16[768,768]{1,0:T(8,128)(2,1)} %get-tuple-element.22.refs_0_, bf16[768,768]{1,0:T(8,128)(2,1)} %collective-permute-done.refs_1_, ...), custom_call_target="tpu_custom_call" | custom-call | flops 38654705664 | bytes 37748736 | tf_op jit(solution)/shard_map/place/pallas_call | solution.py:253
  238.0 9.5 %all-reduce.4.cloned.1.call-done = f32[512,128]{1,0:T(8,128)} async-done(((f32[512,128]{1,0:T(8,128)}), f32[512,128]{1,0:T(8,128)}) %all-reduce.4.cloned.1.call-update) | async-done | bytes 262160 | tf_op jit(solution)/shard_map/psum | solution.py:883
  247.5 1.9 subtract_multiply_fusion
  (2 shorter events, 0.0 us)
Async XLA Ops:
  7.2 240.3 %all-reduce.4.cloned.1.call-start = ((), (), s32[]{:S(2)}) async-start(), calls=%async_computation | async-start | bytes 524288 | tf_op jit(solution)/shard_map/psum | solution.py:883
  8.6 3.0 %copy-start.5 = (f32[1536]{0:T(1024)S(1)}, f32[1536]{0:T(1024)}, u32[]{:S(2)}) copy-start(f32[1536]{0:T(1024)} %param.13) | copy-start | bytes 18436
  184.2 39.5 %collective-permute-start = (bf16[768,768]{1,0:T(8,128)(2,1)}, bf16[768,768]{1,0:T(8,128)(2,1)}, u32[]{:S(2)}, u32[]{:S(2)}) collective-permute-start(bf16[768,768]{1,0:T(8,128)(2,1)} %get-tuple-element.22.refs_0_), channel_id=1, source_target_pairs={{0,8},{8,0},{16,24},{24,16},{1,9},{9,1},{17,25},{25,17},{2,10},{10... | collective-permute-start | bytes 3538952 | tf_op jit(solution)/shard_map/ppermute | solution.py:812
  184.3 28.7 %collective-permute-start.1 = (bf16[768,768]{1,0:T(8,128)(2,1)}, bf16[768,768]{1,0:T(8,128)(2,1)}, u32[]{:S(2)}, u32[]{:S(2)}) collective-permute-start(bf16[768,768]{1,0:T(8,128)(2,1)} %get-tuple-element.22.refs_0_), channel_id=1, source_target_pairs={{0,16},{8,24},{16,0},{24,8},{1,17},{9,25},{17,1},{25,9},{2,18},{10... | collective-permute-start | bytes 3538952 | tf_op jit(solution)/shard_map/ppermute | solution.py:812
  185.9 2.1 copy-start.2
  185.9 2.3 copy-start.3
  188.2 1.9 copy-start.1
  190.1 1.0 copy-start
  190.1 1.0 copy-start.4
  213.0 10.8 %collective-permute-start.2 = (bf16[768,768]{1,0:T(8,128)(2,1)}, bf16[768,768]{1,0:T(8,128)(2,1)}, u32[]{:S(2)}, u32[]{:S(2)}) collective-permute-start(bf16[768,768]{1,0:T(8,128)(2,1)} %collective-permute-done.1.refs_2_), channel_id=1, source_target_pairs={{0,8},{8,0},{16,24},{24,16},{1,9},{9,1},{17,25},{25,17},{2,10},{10... | collective-permute-start | bytes 3538952 | tf_op jit(solution)/shard_map/ppermute | solution.py:812
Sparse Core Ops, SparseCore 0:
  213.2 34.2 all-reduce.3

commit v3 on v2

--- a/solution.py
+++ b/solution.py
@@ -193,7 +193,6 @@
     )
     return (in_weight, out_weight, check_logits)
 
-
 TAIL_LOG2 = (
     -0.9999999403953552,
     -1.1511064767837524,
@@ -218,48 +217,36 @@
     return jnp.maximum(value, 0.0) - size * jnp.exp2(power)
 
 
-def place_kernel(axis, place_ref, own_ref, early_ref, *refs):
-    late_refs, out_ref = refs[:-1], refs[-1]
+def place_kernel(axis, place_ref, own_ref, arrived_ref, out_ref):
     col = place_ref[0]
-    step = pl.program_id(0)
-    rows, cols = own_ref.shape[1:]
-
-    def window(index):
-        start = pl.multiple_of(index * (rows, cols)[axis], 128)
-        return pl.ds(start, (rows, cols)[axis])
-
-    if axis == 1:
-        out_ref[:, window(col)] = own_ref[0]
-        out_ref[:, window(1 - col)] = early_ref[0]
-        return
-    out_ref[window(col)] = own_ref[0]
-    out_ref[window(1 - col), : cols // 2] = early_ref[0]
-    for number, late_ref in enumerate(late_refs):
-        @pl.when(step == number)
-        def _(late_ref=late_ref):
-            out_ref[window(1 - col), cols // 2 :] = late_ref[...]
-
-
-def place_tiles(old, arrived, axis, late=()):
+    extent = own_ref.shape[1 + axis]
+    for index, tile_ref in ((col, own_ref), (1 - col, arrived_ref)):
+        window = pl.ds(pl.multiple_of(index * extent, 128), extent)
+        if axis == 0:
+            out_ref[window] = tile_ref[0]
+        else:
+            out_ref[:, window] = tile_ref[0]
+
+
+def place_tiles(old, arrived, axis):
     count = arrived.shape[0]
     _, rows, cols = old.shape
-    place = jnp.stack([lax.axis_index("col"), lax.axis_index("rep")]).astype(jnp.int32)
+    place = lax.axis_index("col").astype(jnp.int32)[None]
     if axis == 0:
         out_shape, out_block = (2 * rows, count * cols), (2 * rows, cols)
-        out_map = lambda i, place: (0, place[1] ^ i)
+        out_map = lambda i, place: (0, i)
     else:
         out_shape, out_block = (count * rows, 2 * cols), (rows, 2 * cols)
-        out_map = lambda i, place: (place[1] ^ i, 0)
+        out_map = lambda i, place: (i, 0)
     return pl.pallas_call(
         functools.partial(place_kernel, axis),
         grid_spec=pltpu.PrefetchScalarGridSpec(
             num_scalar_prefetch=1,
             grid=(count,),
             in_specs=[
-                pl.BlockSpec((1, rows, cols), lambda i, place: (place[0] * count + (place[1] ^ i), 0, 0)),
-                pl.BlockSpec((1,) + arrived.shape[1:], lambda i, place: (place[1] ^ i, 0, 0)),
-            ]
-            + [pl.BlockSpec(piece.shape, lambda i, place: (0, 0)) for piece in late],
+                pl.BlockSpec((1, rows, cols), lambda i, place: (place[0] * count + i, 0, 0)),
+                pl.BlockSpec((1,) + arrived.shape[1:], lambda i, place: (i, 0, 0)),
+            ],
             out_specs=pl.BlockSpec(out_block, out_map),
         ),
         out_shape=jax.ShapeDtypeStruct(out_shape, old.dtype),
@@ -268,15 +255,16 @@
             flops=2 * rows * cols * count * 4096, bytes_accessed=8 * rows * cols * count, transcendentals=0
         ),
         name="place",
-    )(place, old, arrived, *late)
+    )(place, old, arrived)
 
 
 MESH = pl.DeviceIdType.MESH
 STRIPS = 12
 PAIR = 2
 ROWS = 4
-PASSES = 6
-TICK_PASSES = (19,)
+PASSES = 12
+LAG = 2
+TICK_PASSES = (18, 19, 20)
 
 
 def column(row, rows=128):
@@ -284,18 +272,18 @@
 
 
 def gather_kernel(
-    patch_size, tok_ref, weight_ref, embed_bias_ref, gain_ref, bias_ref, old_in, old_out,
-    embedded_out, in_tiles, in_late, out_tiles, near_kept, near_late, far_got, late_got,
-    kept, far_sent, late_sent, sum_kept, sum_late, near, far, lifted, embedded, part, from_outer, from_inner, middle, final, maps, toks, scales, held,
+    patch_size, tok_ref, weight_ref, rows_ref, check_ref, bias_ref, old_in, old_out,
+    in_tiles, out_tiles, logits_ref,
+    shares, side_check, shares_sent, shares_in, ends, ends_in, check_hi, check_lo, far_got, late_got, kept, far_sent, late_sent, sum_kept, sum_late, near, far, lifted, embedded, part, from_outer, from_inner, middle, final, maps, toks, scales, held,
     sums, sums_in, stats, stats_in, scale_sent, scale_in,
-    near_sem, tile_sem, embed_sem, sums_sem, stats_sem, scale_sem, far_sem, tok_sem, outer_sem, middle_sem,
+    near_sem, tile_sem, sums_sem, stats_sem, scale_sem, far_sem, tok_sem, outer_sem, middle_sem,
     final_sem, keep_sem, across_sem, core_sem, relay_sem, out_sem, out_across_sem, out_core_sem, out_relay_sem,
-    kept_sem, got_sem, sum_sem, in_sem,
+    kept_sem, got_sem, in_sem, shares_sem, ends_sem,
 ):
     rep, row, col = lax.axis_index("rep"), lax.axis_index("row"), lax.axis_index("col")
     owners, strips, depth, width = maps.shape
     half_rows = depth // 2
-    early = in_tiles.shape[2] // width
+    early = strips // 2
     row_count = ROWS
     out_rows = out_tiles.shape[1] // PASSES
     features = weight_ref.shape[1] * row_count
@@ -342,12 +330,6 @@
     def send_late():
         return remote(late_sent, late_got, got_sem.at[1], far_col)
 
-    def keep_sum():
-        return pltpu.make_async_copy(sum_kept, near_kept, sum_sem.at[0])
-
-    def keep_late_sum():
-        return pltpu.make_async_copy(sum_late, near_late, sum_sem.at[1])
-
     def send_far(strip):
         source = old_in.at[(1 - col) * owners + rep, :, columns(strip)]
         return remote(source, far.at[strip], far_sem.at[strip], far_col)
@@ -355,9 +337,6 @@
     def keep_tile(strip):
         return pltpu.make_async_copy(far.at[strip], in_tiles.at[rep, :, columns(strip)], tile_sem.at[strip])
 
-    def keep_late(strip):
-        return pltpu.make_async_copy(far.at[strip], in_late.at[:, columns(strip - early)], tile_sem.at[strip])
-
     def in_across(strip):
         return remote(far.at[strip], in_tiles.at[rep, :, columns(strip)], in_sem.at[strip, 0], far_rep)
 
@@ -377,11 +356,14 @@
     def send_stats(step):
         return remote(stats, stats_in.at[step], stats_sem.at[step], row_peers[step])
 
+    def send_shares(step):
+        return remote(shares_sent, shares_in.at[step], shares_sem.at[step], row_peers[step])
+
+    def send_ends(step):
+        return remote(ends, ends_in.at[step], ends_sem.at[step], row_peers[step])
+
     def send_scale():
         return remote(scale_sent, scale_in, scale_sem, far_col)
-
-    def keep_embedded():
-        return pltpu.make_async_copy(embedded, embedded_out, embed_sem)
 
     def out_block(owner, index):
         return out_tiles.at[owner, pl.ds(index * out_rows, out_rows)]
@@ -442,12 +424,12 @@
     weight_sums = lax.dot_general(
         ones, weight_ref[...], (((1,), (1,)), ((), ())), preferred_element_type=jnp.float32
     )
-    sums[...] = jnp.where(lane == patch_size, jnp.sum(embed_bias_ref[...]), weight_sums)
+    sums[...] = jnp.where(lane == patch_size, jnp.sum(rows_ref[:1]), weight_sums)
     for step in range(row_count - 1):
         send_sums(step).start()
     toks[0] = tok_ref[...]
     embedded[...] = (
-        jnp.dot(tok_ref[...], weight_ref[...], preferred_element_type=jnp.float32) + embed_bias_ref[...]
+        jnp.dot(tok_ref[...], weight_ref[...], preferred_element_type=jnp.float32) + rows_ref[:1]
     )
     values = embedded[...]
     lane = lax.broadcasted_iota(jnp.int32, (values.shape[0], 128), 1)
@@ -456,8 +438,11 @@
     stats[...] = jnp.transpose(jnp.where(lane == 0, total, squares))[:8]
     for step in range(row_count - 1):
         send_stats(step).start()
-    keep_embedded().start()
-
+
+    check = check_ref[...].astype(jnp.float32) * column(rows_ref[2:3])
+    check_hi[...] = check.astype(check_hi.dtype)
+    check_lo[...] = (check - check_hi[...].astype(jnp.float32)).astype(check_lo.dtype)
+    side_check[...] = jnp.broadcast_to(jnp.sum(check, axis=0, keepdims=True), side_check.shape)
     for step in range(row_count - 1):
         send_sums(step).wait_recv()
     mean = column((sums[...] + sums_in[0] + sums_in[1] + sums_in[2])[:1] / features)[:, :1]
@@ -466,9 +451,9 @@
     for half in range(2):
         window = slice(half * extent, (half + 1) * extent)
         raw = jnp.where(
-            number == patch_size, embed_bias_ref[:, window], weight_ref[:, window].astype(jnp.float32)
+            number == patch_size, rows_ref[:1, window], weight_ref[:, window].astype(jnp.float32)
         )
-        lifted[half] = ((raw - mean) * gain_ref[:, window]).astype(lifted.dtype)
+        lifted[half] = ((raw - mean) * rows_ref[1:2, window]).astype(lifted.dtype)
 
     for step in range(row_count - 1):
         send_stats(step).wait_recv()
@@ -488,15 +473,12 @@
         fetch_near(strip).wait()
         send_far(strip).wait_recv()
 
+        keep_tile(strip).start()
+        in_core(strip).start()
+
         @pl.when(strip < early)
         def _():
-            keep_tile(strip).start()
             in_across(strip).start()
-            in_core(strip).start()
-
-        @pl.when(strip >= early)
-        def _():
-            keep_late(strip).start()
 
         total = jnp.dot(lifted[col], near[strip], preferred_element_type=jnp.float32) + jnp.dot(
             lifted[1 - col], far[strip], preferred_element_type=jnp.float32
@@ -598,9 +580,9 @@
             send_out(index).wait_recv()
             out_across(index).start()
             out_core(index).start()
-        if index:
-            out_across(index - 1).wait_recv()
-            out_relay(index - 1).start()
+        if index >= LAG:
+            out_across(index - LAG).wait_recv()
+            out_relay(index - LAG).start()
 
     stages = (
         (0, multiply), (1, halfway), (2, finish), (3, settle), (5, settle_outer), (7, hand_on), (9, activate_near)
@@ -639,7 +621,7 @@
     scales[1] = column(scale_in[:1])
     pieces = blocks * owners
     with_passes(
-        pieces, 1, (pieces // 4, 2 * pieces // 3, pieces - 1),
+        pieces, 3, (2, 6, 10, 14, 18, 22),
         lambda number: activate(number // owners, number % owners, 1),
     )
     for owner in range(owners):
@@ -654,47 +636,101 @@
 
         return step
 
+    for step in range(row_count - 1):
+        send_sums(step).wait_send()
+        send_stats(step).wait_send()
     sum_kept[...] = jnp.zeros_like(sum_kept)
-    with_passes(owners, 4, (owners - 1,), add_up(1, sum_kept))
+    with_passes(owners, 9, (0, owners - 1), add_up(1, sum_kept))
     far_sent[...] = sum_kept[...].astype(far_sent.dtype)
     send_sum().start()
     sum_kept[...] = jnp.zeros_like(sum_kept)
-    with_passes(owners, 5, (0,), add_up(0, sum_kept))
-    keep_sum().start()
+    with_passes(owners, 11, (0,), add_up(0, sum_kept))
 
     fetch_late(rep).start()
-    pass_out(PASSES)
+    for strip in range(strips // 2, strips):
+        in_across(strip).start()
     for index in range(PASSES):
         out_core(index).wait_recv()
-    for turn in (1, 2):
-        fetch_late(owner_of(turn)).start()
-    for index in range(PASSES):
-        out_relay(index).wait_recv()
-    fetch_late(owner_of(owners - 1)).start()
-    for owner in range(owners):
-        fetch_late(owner).wait()
+    fetch_late(owner_of(2)).start()
+    for index in range(PASSES, PASSES + LAG):
+        pass_out(index)
+    fetch_late(owner_of(1)).start()
     sum_late[...] = jnp.zeros_like(sum_late)
-    with_passes(owners, 0, (), add_up(1, sum_late))
+
+    def add_late(number, carry):
+        turn = number % 2 * 2 + number // 2
+        fetch_late(owner_of(turn)).wait()
+
+        @pl.when(number == 1)
+        def _():
+            for index in range(PASSES):
+                out_relay(index).wait_recv()
+            fetch_late(owner_of(owners - 1)).start()
+
+        add_up(1, sum_late)(turn)
+        return carry
+
+    lax.fori_loop(0, owners, add_late, 0)
     late_sent[...] = sum_late[...].astype(late_sent.dtype)
     send_late().start()
     sum_late[...] = jnp.zeros_like(sum_late)
     with_passes(owners, 0, (), add_up(0, sum_late))
-    keep_late_sum().start()
+
+    def update(half, total, got):
+        window = pl.ds(pl.multiple_of(half * extent, extent), extent)
+        updated = embedded[:, window] + total[...] + got[...].astype(jnp.float32) + rows_ref[3:4, window]
+        upper = updated.astype(jnp.bfloat16)
+        lower = (updated - upper.astype(jnp.float32)).astype(jnp.bfloat16)
+        logits = (
+            jnp.dot(upper, check_hi[window], preferred_element_type=jnp.float32)
+            + jnp.dot(lower, check_hi[window], preferred_element_type=jnp.float32)
+            + jnp.dot(upper, check_lo[window], preferred_element_type=jnp.float32)
+        )
+        total = jnp.sum(updated, axis=1, keepdims=True)
+        squares = jnp.sum(updated * updated, axis=1, keepdims=True)
+        return logits, jnp.where(lane == 0, total, squares)
+
+    send_sum().wait_recv()
+    logits, sides = update(1 - col, sum_late, far_got)
+    shares[...] = logits
+    stats[...] = jnp.transpose(sides)[:8]
+    send_late().wait_recv()
+    logits, sides = update(col, sum_kept, late_got)
+    shares[...] += logits
+    local = weight_ref.shape[1]
+    ends[...] = stats[...] + jnp.transpose(sides)[:8]
+    ends[2:3, :128] = side_check[:1]
+    centered = shares[...] - column(ends[:1] / local) * side_check[:1]
+    shares_sent[...] = centered.astype(shares_sent.dtype)
+    for step in range(row_count - 1):
+        send_ends(step).start()
+        send_shares(step).start()
+    for step in range(row_count - 1):
+        send_ends(step).wait_recv()
+    every = [ends[...]] + [ends_in[step] for step in range(row_count - 1)]
+    moments = sum(every[1:], every[0]) / features
+    mean = moments[:1]
+    scale = column(lax.rsqrt(moments[1:2] - mean * mean + EPSILON))
+    for side in every:
+        centered = centered + column(side[:1] / local - mean) * side[2:3, :128]
+    for step in range(row_count - 1):
+        send_shares(step).wait_recv()
+        centered = centered + shares_in[step].astype(jnp.float32)
+    logits_ref[...] = scale * centered
+    for step in range(row_count - 1):
+        send_ends(step).wait_send()
+        send_shares(step).wait_send()
+    for strip in range(strips // 2, strips):
+        in_across(strip).wait_recv()
+        in_relay(strip).start()
 
     def finish_strip(strip, carry):
         for copy in (across(strip), to_core(strip), relay(strip), send_far(strip)):
             copy.wait_send()
-
-        @pl.when(strip < early)
-        def _():
-            keep_tile(strip).wait()
-            in_core(strip).wait()
-            in_relay(strip).wait()
-            in_across(strip).wait_send()
-
-        @pl.when(strip >= early)
-        def _():
-            keep_late(strip).wait()
+        keep_tile(strip).wait()
+        in_core(strip).wait()
+        in_relay(strip).wait()
+        in_across(strip).wait_send()
 
         @pl.when(outer)
         def _():
@@ -710,22 +746,16 @@
 
     lax.fori_loop(0, strips, finish_strip, 0)
 
-    keep_sum().wait()
-    keep_late_sum().wait()
-    for step in range(row_count - 1):
-        send_sums(step).wait_send()
-        send_stats(step).wait_send()
-    keep_embedded().wait()
     for copy in (send_scale(), send_tok()):
         copy.wait_send()
     for index in range(PASSES):
         for copy in (send_out(index), out_across(index), out_core(index), out_relay(index)):
             copy.wait_send()
-    send_sum().wait()
-    send_late().wait()
-
-
-def gather_hidden(patch_size, tok, weight, embed_bias, gain, in_bias, old_in, old_out):
+    send_sum().wait_send()
+    send_late().wait_send()
+
+
+def gather_hidden(patch_size, tok, weight, rows, check_weight, in_bias, old_in, old_out):
     rep_count = lax.axis_size("rep")
     tokens, depth = tok.shape
     local = weight.shape[1]
@@ -740,18 +770,23 @@
     return pl.pallas_call(
         functools.partial(gather_kernel, patch_size),
         out_shape=(
-            jax.ShapeDtypeStruct((tokens, local), f32),
-            jax.ShapeDtypeStruct((rep_count, tile_rows, group_cols // 2), old_in.dtype),
-            jax.ShapeDtypeStruct((tile_rows, group_cols // 2), old_in.dtype),
+            jax.ShapeDtypeStruct((rep_count, tile_rows, group_cols), old_in.dtype),
             jax.ShapeDtypeStruct((rep_count,) + old_out.shape[1:], old_out.dtype),
-            jax.ShapeDtypeStruct((tokens, tile_rows), f32),
-            jax.ShapeDtypeStruct((tokens, tile_rows), f32),
-            jax.ShapeDtypeStruct((tokens, tile_rows), bf16),
-            jax.ShapeDtypeStruct((tokens, tile_rows), bf16),
+            jax.ShapeDtypeStruct((tokens, 128), f32),
         ),
         in_specs=[vmem] * 5 + [any_space] * 2,
-        out_specs=(any_space,) * 8,
+        out_specs=(any_space, any_space, vmem),
         scratch_shapes=[
+            pltpu.VMEM((tokens, 128), f32),
+            pltpu.VMEM((8, 128), f32),
+            pltpu.VMEM((tokens, 128), bf16),
+            pltpu.VMEM((ROWS - 1, tokens, 128), bf16),
+            pltpu.VMEM((8, tokens), f32),
+            pltpu.VMEM((ROWS - 1, 8, tokens), f32),
+            pltpu.VMEM((local, 128), bf16),
+            pltpu.VMEM((local, 128), bf16),
+            pltpu.VMEM((tokens, tile_rows), bf16),
+            pltpu.VMEM((tokens, tile_rows), bf16),
             pltpu.VMEM((rep_count,) + old_out.shape[1:], old_out.dtype),
             pltpu.VMEM((tokens, tile_rows), bf16),
             pltpu.VMEM((tokens, tile_rows), bf16),
@@ -778,7 +813,6 @@
             pltpu.VMEM((8, tokens), f32),
             dma((STRIPS,)),
             dma((STRIPS,)),
-            dma,
             dma((ROWS - 1, 2)),
             dma((ROWS - 1, 2)),
             dma((2,)),
@@ -797,23 +831,16 @@
             dma((PASSES, 2)),
             dma((rep_count,)),
             dma((2, 2)),
-            dma((2,)),
-            dma((STRIPS // 2, 3, 2)),
+            dma((STRIPS, 3, 2)),
+            dma((ROWS - 1, 2)),
+            dma((ROWS - 1, 2)),
         ],
         compiler_params=pltpu.CompilerParams(
             collective_id=0, has_side_effects=True, vmem_limit_bytes=66_000_000
         ),
         cost_estimate=pl.CostEstimate(flops=10**10, bytes_accessed=10**8, transcendentals=0),
         name="gather_hidden",
-    )(tok, weight, embed_bias[None], gain[None], in_bias.reshape(-1, 1, PAIR * width), old_in, old_out)
-
-
-def rep_partner(value, mask):
-    return lax.ppermute(value, "rep", [(s, s ^ mask) for s in range(lax.axis_size("rep"))])
-
-
-def after(value, *others):
-    return lax.optimization_barrier((value,) + others)[0]
+    )(tok, weight, rows, check_weight, in_bias.reshape(-1, 1, PAIR * width), old_in, old_out)
 
 
 def row_of(restore_id, table):
@@ -833,17 +860,17 @@
     final_gain,
     check_weight,
 ):
-    col = lax.axis_index("col")
-    row_count = lax.axis_size("row")
+    col, rep = lax.axis_index("col"), lax.axis_index("rep")
+    rep_count, row_count = lax.axis_size("rep"), lax.axis_size("row")
+    tile_rows = old_in.shape[1]
     token_count, patch_size = patches.shape
     feature_count = embed_weight.shape[1] * row_count
     depth = -(-(patch_size + 1) // 32) * 32
 
-    layer_gain = row_of(restore_id, norm_gains)
     in_bias = row_of(restore_id, in_biases)
-    out_bias = row_of(restore_id, out_biases)
-
-    check32 = check_weight.astype(jnp.float32) * final_gain[:, None]
+    rows = jnp.stack(
+        (embed_bias, row_of(restore_id, norm_gains), final_gain, row_of(restore_id, out_biases))
+    )
     tok = jnp.concatenate(
         (
             patches,
@@ -853,44 +880,10 @@
         axis=1,
     )
     weight = jnp.pad(embed_weight, ((0, depth - patch_size), (0, 0)))
-    embedded, in_tiles, in_late, out_tiles, near_kept, near_late, far_got, late_got = gather_hidden(
-        patch_size, tok, weight, embed_bias, layer_gain, in_bias, old_in, old_out
-    )
-    late_across = rep_partner(in_late, 2)
-    late_core = rep_partner(in_late, 1)
-    branch_parts = (
-        near_kept + late_got.astype(jnp.float32),
-        near_late + far_got.astype(jnp.float32),
-    )
-    branch = jnp.where(
-        col == 0, jnp.concatenate(branch_parts, axis=1), jnp.concatenate(branch_parts[::-1], axis=1)
-    )
-    updated = embedded + branch + out_bias
-
-    def halves(value):
-        upper = lax.reduce_precision(value, 8, 7)
-        return upper.astype(jnp.bfloat16), (value - upper).astype(jnp.bfloat16)
-
-    updated_hi, updated_lo = halves(updated)
-    check_hi, check_lo = halves(check32)
-    raw = (
-        jnp.dot(updated_hi, check_hi, preferred_element_type=jnp.float32)
-        + jnp.dot(updated_lo, check_hi, preferred_element_type=jnp.float32)
-        + jnp.dot(updated_hi, check_lo, preferred_element_type=jnp.float32)
-    )
-    shares = (raw, jnp.sum(updated, axis=1), jnp.sum(updated * updated, axis=1))
-    out_tiles = after(out_tiles, *shares)
-    raw = lax.psum(shares[0], "row")
-    total, squares = lax.psum(shares[1:], "row")
-    check_sum = lax.psum(jnp.sum(check32, axis=0), "row")
-    out_weight = place_tiles(old_out, out_tiles, 1)
-    late_relay = rep_partner(after(late_across, out_weight), 1)
-    in_weight = place_tiles(old_in, in_tiles, 0, (in_late, late_core, late_across, late_relay))
-    raw, in_weight, out_weight = lax.optimization_barrier((raw, in_weight, out_weight))
-    average = (total / feature_count)[:, None]
-    spread = (squares / feature_count)[:, None] - average * average
-    check_logits = lax.rsqrt(spread + EPSILON) * (raw - average * check_sum)
-    return (in_weight, out_weight, check_logits)
+    in_tiles, out_tiles, check_logits = gather_hidden(
+        patch_size, tok, weight, rows, check_weight, in_bias, old_in, old_out
+    )
+    return (place_tiles(old_in, in_tiles, 0), place_tiles(old_out, out_tiles, 1), check_logits)
 
 
 def on_either(*args):

time: 257 us -> 219 us (0.85)
  waiting for transfers between devices: 14.8 us -> 0 us
  between operations: 14.8 us -> 1.45 us
  Pallas kernels: 195 us -> 208 us
  blocking collectives: 10.4 us -> 0 us
  other arithmetic: 6.53 us -> 1.64 us
  local copies, waits for them, and re-layouts: 10.3 us -> 7.36 us
  matrix products: 2.78 us -> 0 us
    pallas_call x1, Pallas kernels: 167 us -> 183 us  [gather_hidden(): pl.pallas_call(functools.partial(gather_kernel, patch_size), out_shape=(j...]
    psum x1 -> x0, blocking collectives: 10.4 us -> none  [fast_device(): check_sum = lax.psum(jnp.sum(check32, axis=0), 'row')]
    psum x1 -> x0, waiting for transfers between devices: 9.53 us -> none  [fast_device(): raw = lax.psum(shares[0], 'row')]
    ppermute x3 -> x0, waiting for transfers between devices: 5.21 us -> none  [rep_partner(): lax.ppermute(value, 'rep', [(s, s ^ mask) for s in range(lax.axis_size('r...]
    dot_general x3 -> x0, matrix products: 2.78 us -> none  [the longest x1 1.41 us: fast_device(): jnp.dot(updated_lo, check_hi, preferred_element_type=jnp.float32)]
  transfers between devices with their start and end apart: 4 -> 0, of which waited for: 2 -> 0; matrix products, arithmetic and copies ran while one was open for 3% -> 0% of each run, Pallas kernels for 11% -> 0%
where the time goes in v3:
time: 219 us
  Pallas kernels  208 us (95%)
  local copies, waits for them, and re-layouts  7.36 us (3%)
    pallas_call x1, Pallas kernels, gather_hidden(): pl.pallas_call(functools.partial(gather_kernel, patch_size), out_shape=(j...  183 us
    pallas_call x2, Pallas kernels, place_tiles(): pl.pallas_call(functools.partial(place_kernel, axis), grid_spec=pltpu.Pre...  25.3 us

profile of v3, /device:TPU:0, one launch (start us, length us, event | category | flops | bytes accessed | tf_op | source)
XLA Modules:
  0.0 218.6 jit_solution(8924408998363716337)
XLA Ops:
  0.6 0.0 copy-start
  1.4 0.1 pad.11.clone
  1.5 0.1 pad.10.clone
  1.6 0.7 stack.9
  2.3 0.7 stack.10
  3.0 0.8 constant_dynamic-slice_fusion.1
  3.8 0.6 pad_maximum_fusion.rows_ref
  4.5 1.5 constant_dynamic-slice_fusion
  6.0 1.4 copy.14
  7.4 1.0 maximum_maximum_fusion.tok_ref
  8.4 0.0 copy-done
  8.4 1.4 pad.4.weight_ref
  9.7 182.9 %gather_hidden.1 = (bf16[4,768,1536]{2,1,0:T(8,128)(2,1)}, bf16[4,1536,768]{2,1,0:T(8,128)(2,1)}, f32[512,128]{1,0:T(8,128)}) custom-call(bf16[512,608]{1,0:T(8,128)(2,1)} %maximum_maximum_fusion.tok_ref, bf16[608,1536]{1,0:T(8,128)(2,1)} %pad.4.weight_ref, f32[4,1536]{1,0:T(4,128)} %pad_maximum_fusion.rows_ref, bf16[1536,128]{1,0:T(8,128)(2,1)} %check_ref.1, ...), custom_call_target="tpu_custom_call" | custom-call | flops 10000000000 | bytes 100000000 | tf_op jit(solution)/shard_map/gather_hidden/pallas_call | solution.py:770
  192.6 12.6 %place.2 = bf16[1536,6144]{1,0:T(8,128)(2,1)} custom-call(s32[1]{0:T(128)} %bitcast.place_ref, bf16[8,768,1536]{2,1,0:T(8,128)(2,1)} %own_ref.2, bf16[4,768,1536]{2,1,0:T(8,128)(2,1)} %get-tuple-element.6.arrived_ref), custom_call_target="tpu_custom_call" | custom-call | flops 38654705664 | bytes 37748736 | tf_op jit(solution)/shard_map/place/pallas_call | solution.py:241
  205.3 0.0 copy-start.1
  205.3 12.7 %place.3 = bf16[6144,1536]{1,0:T(8,128)(2,1)} custom-call(s32[1]{0:T(128)} %bitcast.place_ref, bf16[8,1536,768]{2,1,0:T(8,128)(2,1)} %own_ref.3, bf16[4,1536,768]{2,1,0:T(8,128)(2,1)} %get-tuple-element.7.arrived_ref), custom_call_target="tpu_custom_call" | custom-call | flops 38654705664 | bytes 37748736 | tf_op jit(solution)/shard_map/place/pallas_call | solution.py:241
  217.9 0.0 copy-done.1
  217.9 0.7 copy.17
  (1 shorter events, 0.0 us)
Async XLA Ops:
  0.6 7.7 %copy-start = (bf16[588,1536]{1,0:T(8,128)(2,1)S(1)}, bf16[588,1536]{1,0:T(8,128)(2,1)}, u32[]{:S(2)}) copy-start(bf16[588,1536]{1,0:T(8,128)(2,1)} %param.12) | copy-start | bytes 5419012
  205.3 12.7 %copy-start.1 = (f32[512,128]{1,0:T(8,128)S(1)}, f32[512,128]{1,0:T(8,128)}, u32[]{:S(2)}) copy-start(f32[512,128]{1,0:T(8,128)} %get-tuple-element.16) | copy-start | bytes 786436
